TPU v7x, 256 devices: a whole 4x4x8 slice. The times are simulated.
256 devices in a mesh: dp: 8 (over z), table: 32 (over y, x, core).
Axes of the slice: x: 4, y: 4, z: 8, core: 2. Of those that a mesh axis runs over, the one named last changes fastest.
Arguments:
- queries: bfloat16 [32768, 2, 512], P(('dp', 'table')), may hold values from -6 to 6
- sub_keys: bfloat16 [2, 2, 512, 256], replicated, may hold values from -0.375 to 0.375
- values: bfloat16 [512, 512, 1024], P('table', None, 'dp'), may hold values from -0.1875 to 0.1875
- slot_first: int32 [32768, 2, 4], P(('dp', 'table')), may hold values from 0 to 511, as said below
- slot_second: int32 [32768, 2, 4], P(('dp', 'table')), may hold values from 0 to 511
- cotangent: bfloat16 [32768, 1024], P(('dp', 'table')), may hold values from -6 to 6
Outputs:
- value_update: float32 [512, 512, 1024], P('table', None, 'dp')
- key_update: float32 [2, 2, 512, 256], P(None, None, ('dp', 'table'))
- clip_factor: float32 [1], replicated
Inputs may be any that keep to these rules, and one draw needn't show every extreme that they name: Within each aligned block of 128 tokens (the tokens of one device), at most 48 of its 1024 slots have slot_first in any one range [r * 16, (r + 1) * 16), and exactly 48 do in one such range.
All inputs are finite; a program needn't handle non-finite values.
Results may differ from a plain program's by a relative error of at most 0.0003.
Values may be sent and summed in bfloat16 or wider, within the bound.
No kernel may reach another device: no remote copies, remote signals or barrier semaphores. Data moves between devices by JAX's collectives and lax.ppermute only.
A program may use at most 64 MiB of HBM per device.

v0:
```python
import functools
import math

import jax
import jax.numpy as jnp
from jax import lax
from jax.experimental import pallas as pl
from jax.experimental.pallas import tpu as pltpu
from jax.sharding import Mesh
from jax.sharding import PartitionSpec as P


TABLE = ("table_0", "table_1", "table_2")
DP_TABLE = ("dp", "table_0", "table_1", "table_2")
CHIPS = ("dp", "table_0", "table_1")
NSUB = 512
BLK = 16
CAP = 48
OWN = 32
NDP = 8
TOK = 128
PICKS = 8
HALF = 256
KEYS = NSUB // NDP
LISTS = OWN * NDP
PART = NDP // 2
PART_LISTS = OWN * PART
ROWS = BLK * NSUB
RECORDS = 2 * NDP
ACCS = 8
BATCH = 4
EXTRA = 16
F32 = jnp.float32
BF16 = jnp.bfloat16
LIMIT_RATIO = 5.0

NT = (((1,), (1,)), ((), ()))
NN = (((1,), (0,)), ((), ()))

PARAMS = pltpu.CompilerParams(vmem_limit_bytes=20 * 1024 * 1024)


def pieces(x):
    high = x.astype(BF16)
    rest = x - high.astype(F32)
    mid = rest.astype(BF16)
    low = (rest - mid.astype(F32)).astype(BF16)
    return high, mid, low


def joined(high, mid, low):
    return (high.astype(F32) + mid.astype(F32)) + low.astype(F32)


def vmem(count):
    return [pl.BlockSpec(memory_space=pltpu.VMEM)] * count


def smem():
    return [pl.BlockSpec(memory_space=pltpu.SMEM)]


def shape(dims, kind):
    return jax.ShapeDtypeStruct(dims, kind)


def prep_kernel(q_ref, keys_ref, first_ref, second_ref, cot_ref, out_ref, late_ref):
    first = first_ref[...]
    second = second_ref[...]
    key_id = lax.broadcasted_iota(jnp.int32, (NSUB, TOK), 0)
    scores = [None] * PICKS
    for half, index in ((0, first), (1, second)):
        for head in range(2):
            at = head * 2 * HALF + half * HALF
            table = lax.dot_general(
                keys_ref[half, head], q_ref[:, at : at + HALF], NT, preferred_element_type=F32
            )
            for k in range(4):
                slot = head * 4 + k
                part = jnp.sum(
                    jnp.where(key_id == index[slot : slot + 1, :], table, 0.0),
                    axis=0,
                    keepdims=True,
                )
                scores[slot] = part if scores[slot] is None else scores[slot] + part
    exps = [jnp.exp(s) for s in scores]
    weights = []
    for head in range(2):
        e = exps[head * 4 : head * 4 + 4]
        total = (e[0] + e[1]) + (e[2] + e[3])
        weights += [x / total for x in e]
    owner = jnp.right_shift(first, 4)
    owner_id = lax.broadcasted_iota(jnp.int32, (OWN, TOK), 0)
    member = [
        jnp.where(owner_id == owner[s : s + 1, :], 1.0, 0.0).astype(F32) for s in range(PICKS)
    ]
    earlier = jnp.where(
        lax.broadcasted_iota(jnp.int32, (TOK, TOK), 0)
        < lax.broadcasted_iota(jnp.int32, (TOK, TOK), 1),
        1.0,
        0.0,
    ).astype(BF16)
    member_all = jnp.concatenate(member, axis=0).astype(BF16)
    ranks = lax.dot_general(member_all, earlier, NN, preferred_element_type=F32)
    base = jnp.zeros((OWN, 1), F32)
    token = lax.broadcasted_iota(jnp.int32, (1, TOK), 1).astype(F32)
    lane_id = lax.broadcasted_iota(jnp.int32, (TOK, TOK), 0)
    planes = [jnp.zeros((OWN, TOK), F32)] * 2
    targets = []
    for s in range(PICKS):
        rank = jnp.sum(
            member[s] * (ranks[s * OWN : (s + 1) * OWN, :] + base), axis=0, keepdims=True
        )
        base = base + jnp.sum(member[s], axis=1, keepdims=True)
        place = rank.astype(jnp.int32)
        row = jnp.bitwise_and(first[s : s + 1, :], BLK - 1) * NSUB + second[s : s + 1, :]
        at_value = lane_id == place
        at_rest = lane_id == place + CAP
        at_token = (
            lane_id == place + 2 * CAP,
            lane_id == jnp.where(place >= TOK - 2 * CAP, place + 4 * CAP - TOK, -1),
        )
        weight = pieces(weights[s])
        parts = (
            (jnp.right_shift(row, 5).astype(F32), jnp.bitwise_and(row, 31).astype(F32)),
            (weight[0].astype(F32), weight[1].astype(F32)),
        )
        chosen = member[s].astype(BF16)
        for p in range(2):
            entry = jnp.where(
                at_value,
                parts[p][0],
                jnp.where(at_rest, parts[p][1], jnp.where(at_token[p], token, 0.0)),
            ).astype(BF16)
            planes[p] = planes[p] + lax.dot_general(
                chosen, entry, NT, preferred_element_type=F32
            )
        targets.append(owner[s : s + 1, :] * TOK + place)
    planes = [plane.astype(BF16) for plane in planes]
    for d in range(NDP):
        out_ref[d, 0:TOK, :] = cot_ref[:, d * TOK : (d + 1) * TOK]
        for p in range(2):
            out_ref[d, TOK + p * OWN : TOK + (p + 1) * OWN, :] = planes[p]
    late_ref[0:TOK, :] = q_ref[...]
    parts = list(pieces(jnp.concatenate(weights, axis=0)))
    for index in (jnp.concatenate(targets, axis=0), first, second):
        parts += [
            jnp.right_shift(index, 6).astype(F32).astype(BF16),
            jnp.bitwise_and(index, 63).astype(F32).astype(BF16),
        ]
    parts = [part.astype(F32) for part in parts]
    parts += [jnp.zeros((PICKS, TOK), F32)] * (EXTRA - len(parts))
    for s in range(PICKS):
        late_ref[TOK : TOK + EXTRA, s * TOK : (s + 1) * TOK] = jnp.concatenate(
            [part[s : s + 1, :] for part in parts], axis=0
        ).astype(BF16)


def prep(q, keys, first, second, cot):
    return pl.pallas_call(
        prep_kernel,
        in_specs=vmem(5),
        out_specs=vmem(2),
        out_shape=(
            shape((NDP, TOK + 2 * OWN, TOK), BF16),
            shape((TOK + EXTRA, 4 * HALF), BF16),
        ),
        compiler_params=PARAMS,
        name="prep",
    )(q, keys, first, second, cot)


def late_index(late_ref, slot, part):
    at = slice(slot * TOK, (slot + 1) * TOK)
    high = late_ref[part : part + 1, at].astype(F32).astype(jnp.int32)
    low = late_ref[part + 1 : part + 2, at].astype(F32).astype(jnp.int32)
    return high * 64 + low


def source(me, k):
    return jnp.bitwise_and(me + NDP - k, NDP - 1)


def expand_kernel(part, sent_ref, out_ref, *scratch):
    lane = lax.broadcasted_iota(jnp.int32, (CAP, TOK), 1)
    for k in range(PART):
        s = part * PART + k
        planes = [sent_ref[s, TOK + p * OWN : TOK + (p + 1) * OWN, :].astype(F32) for p in range(2)]
        columns = [jnp.transpose(jnp.concatenate([plane] * 4, axis=0)) for plane in planes]
        token = jnp.concatenate(
            [columns[0][2 * CAP : TOK, :], columns[1][2 * CAP : 5 * CAP - TOK, :]], axis=0
        ).astype(jnp.int32)
        chosen = jnp.concatenate(
            [
                jnp.where(token[:, o : o + 1] == lane, 1.0, 0.0).astype(BF16)
                for o in range(OWN)
            ],
            axis=0,
        )
        out_ref[:, k * CAP : (k + 1) * CAP, :] = (
            lax.dot_general(chosen, sent_ref[s, 0:TOK, :], NN, preferred_element_type=F32)
            .astype(BF16)
            .reshape(OWN, CAP, TOK)
        )
    if part == 0:
        wide_ref = scratch[0]
        for s in range(NDP):
            for p in range(2):
                wide_ref[:, 2 * s + p, :] = sent_ref[
                    s, TOK + p * OWN : TOK + (p + 1) * OWN, :
                ].astype(F32)
        out_ref[:, PART * CAP :, :] = wide_ref[...].astype(BF16)


def expand(part, sent):
    extra = RECORDS if part == 0 else 0
    return pl.pallas_call(
        functools.partial(expand_kernel, part),
        in_specs=vmem(1),
        out_specs=vmem(1)[0],
        out_shape=shape((OWN, PART * CAP + extra, TOK), BF16),
        scratch_shapes=[pltpu.VMEM((OWN, RECORDS, TOK), F32)] if part == 0 else [],
        compiler_params=PARAMS,
        name="expand",
    )(sent)


def decode_kernel(rows_ref, row_ref, weight_ref, wide_ref):
    for t in range(OWN):
        wide_ref[t * RECORDS : (t + 1) * RECORDS, :] = rows_ref[t, PART * CAP :, :].astype(F32)
    index = wide_ref[pl.ds(0, LISTS, stride=2), :]
    weight = wide_ref[pl.ds(1, LISTS, stride=2), :]
    row_ref[...] = (index * 32.0 + pltpu.roll(index, TOK - CAP, 1)).astype(jnp.int32)
    weight_ref[...] = weight + pltpu.roll(weight, TOK - CAP, 1)


def decode(rows):
    return pl.pallas_call(
        decode_kernel,
        in_specs=vmem(1),
        out_specs=vmem(2),
        out_shape=(shape((LISTS, TOK), jnp.int32), shape((LISTS, TOK), F32)),
        scratch_shapes=[pltpu.VMEM((OWN * RECORDS, TOK), F32)],
        compiler_params=PARAMS,
        name="decode",
    )(rows)


GATHER_LISTS = 32


def gather_kernel(row_ref, table_ref, out_ref, wide_ref, got_ref):
    step = pl.program_id(0)

    @pl.when(step == 0)
    def _():
        def widen(i, carry):
            at = pl.multiple_of(i * 256, 256)
            wide_ref[pl.ds(at, 256), :] = table_ref[pl.ds(at, 256), :].astype(F32)
            return carry

        lax.fori_loop(0, ROWS // 256, widen, 0)

    part = step // (PART_LISTS // GATHER_LISTS)
    first_list = (step % (PART_LISTS // GATHER_LISTS)) * GATHER_LISTS

    def one_list(i, carry):
        at = first_list + i
        which = (at // PART) * NDP + part * PART + at % PART
        for j in range(CAP):
            row = row_ref[which, j]
            got_ref[pl.ds(i * CAP + j, 1), :] = wide_ref[pl.ds(row, 1), :]
        return carry

    lax.fori_loop(0, GATHER_LISTS, one_list, 0)
    out_ref[...] = got_ref[...].astype(BF16)


def gather_rows(row, table):
    return pl.pallas_call(
        gather_kernel,
        grid=(LISTS // GATHER_LISTS,),
        in_specs=smem() + [pl.BlockSpec((ROWS, TOK), lambda g: (0, 0))],
        out_specs=pl.BlockSpec((GATHER_LISTS * CAP, TOK), lambda g: (g, 0)),
        out_shape=shape((LISTS * CAP, TOK), BF16),
        scratch_shapes=[
            pltpu.VMEM((ROWS, TOK), F32),
            pltpu.VMEM((GATHER_LISTS * CAP, TOK), F32),
        ],
        compiler_params=PARAMS,
        name="gather_rows",
    )(row, table)


DOT_OWN = 8


def dots_kernel(part, *refs):
    rows_ref, value_ref = refs[:2]
    out_ref = refs[-1]
    place = lax.broadcasted_iota(jnp.int32, (CAP, TOK), 0)
    lane = lax.broadcasted_iota(jnp.int32, (CAP, TOK), 1)
    own = place == lane
    made = []
    for t in range(DOT_OWN):
        if part == 1:
            made.append(refs[2][t * PART : (t + 1) * PART, :])
        for k in range(PART):
            at = (t * PART + k) * CAP
            product = rows_ref[t, k * CAP : (k + 1) * CAP, :].astype(F32) * value_ref[
                at : at + CAP, :
            ].astype(F32)
            total = jnp.sum(product, axis=1, keepdims=True)
            made.append(jnp.sum(jnp.where(own, total, 0.0), axis=0, keepdims=True))
    out_ref[...] = jnp.concatenate(made, axis=0)


def dots(part, rows, value, earlier=()):
    steps = OWN // DOT_OWN
    count = DOT_OWN * (PART if part == 0 else NDP)
    return pl.pallas_call(
        functools.partial(dots_kernel, part),
        grid=(steps,),
        in_specs=[
            pl.BlockSpec((DOT_OWN, rows.shape[1], TOK), lambda g: (g, 0, 0)),
            pl.BlockSpec((DOT_OWN * PART * CAP, TOK), lambda g: (part * steps + g, 0)),
        ]
        + [pl.BlockSpec((DOT_OWN * PART, TOK), lambda g: (g, 0))] * len(earlier),
        out_specs=pl.BlockSpec((count, TOK), lambda g: (g, 0)),
        out_shape=shape((count * steps, TOK), F32),
        compiler_params=PARAMS,
        name="dots",
    )(rows, value, *earlier)


SCATTER_OWN = 8
SCATTER_STEPS = OWN // SCATTER_OWN


def scatter_kernel(row_ref, weight_ref, rows_a_ref, rows_b_ref, out_ref, sq_ref, wide_ref, *accs):
    step = pl.program_id(0)

    @pl.when(step == 0)
    def _():
        def clear(i, carry):
            at = pl.multiple_of(i * 64, 64)
            for acc in accs:
                acc[pl.ds(at, 64), :] = jnp.zeros((64, TOK), F32)
            return carry

        lax.fori_loop(0, ROWS // 64, clear, 0)

    block = step % SCATTER_STEPS
    part = step // SCATTER_STEPS
    at = pl.multiple_of(block * SCATTER_OWN * NDP, SCATTER_OWN * NDP)
    weight = weight_ref[pl.ds(at, SCATTER_OWN * NDP), :]
    columns = jnp.transpose(jnp.concatenate([weight] * (TOK // (SCATTER_OWN * NDP)), axis=0))
    for which, rows_ref in ((0, rows_a_ref), (1, rows_b_ref)):

        @pl.when(part == which)
        def _():
            for t in range(SCATTER_OWN):
                for k in range(PART):
                    i = t * PART + k
                    s = t * NDP + which * PART + k
                    wide_ref[i * CAP : (i + 1) * CAP, :] = (
                        rows_ref[t, k * CAP : (k + 1) * CAP, :].astype(F32)
                        * columns[0:CAP, s : s + 1]
                    )

    def one_list(i, carry):
        which = (block * SCATTER_OWN + i // PART) * NDP + part * PART + i % PART
        waiting = []
        for b in range(0, CAP, BATCH):
            made = []
            for j in range(b, b + BATCH):
                acc = accs[j % ACCS]
                row = row_ref[which, j]
                made.append((acc, row, acc[pl.ds(row, 1), :] + wide_ref[pl.ds(i * CAP + j, 1), :]))
            for acc, row, total in waiting:
                acc[pl.ds(row, 1), :] = total
            waiting = made
        for acc, row, total in waiting:
            acc[pl.ds(row, 1), :] = total
        return carry

    lax.fori_loop(0, SCATTER_OWN * PART, one_list, 0)

    @pl.when(step == pl.num_programs(0) - 1)
    def _():
        def collect(i, total):
            at = pl.multiple_of(i * 64, 64)
            value = accs[0][pl.ds(at, 64), :]
            for acc in accs[1:]:
                value = value + acc[pl.ds(at, 64), :]
            out_ref[pl.ds(at, 64), :] = value
            square = value * value
            return total + jnp.sum(square.reshape(8, 8, TOK), axis=0)

        sq_ref[...] = lax.fori_loop(0, ROWS // 64, collect, jnp.zeros((8, TOK), F32))


def scatter_rows(row, weight, rows_a, rows_b):
    last = SCATTER_STEPS - 1
    return pl.pallas_call(
        scatter_kernel,
        grid=(2 * SCATTER_STEPS,),
        in_specs=smem()
        + vmem(1)
        + [
            pl.BlockSpec(
                (SCATTER_OWN, rows_a.shape[1], TOK), lambda g: (jnp.minimum(g, last), 0, 0)
            ),
            pl.BlockSpec(
                (SCATTER_OWN, rows_b.shape[1], TOK),
                lambda g: (jnp.maximum(g - SCATTER_STEPS, 0), 0, 0),
            ),
        ],
        out_specs=vmem(2),
        out_shape=(shape((ROWS, TOK), F32), shape((8, TOK), F32)),
        scratch_shapes=[pltpu.VMEM((SCATTER_OWN * PART * CAP, TOK), F32)]
        + [pltpu.VMEM((ROWS, TOK), F32) for _ in range(ACCS)],
        compiler_params=pltpu.CompilerParams(vmem_limit_bytes=52 * 1024 * 1024),
        name="scatter_rows",
    )(row, weight, rows_a, rows_b)


SCALE_ROWS = 1024


def scale_kernel(factor_ref, value_ref, out_ref):
    out_ref[...] = value_ref[...] * factor_ref[0]


def scaled(factor, value):
    return pl.pallas_call(
        scale_kernel,
        grid=(ROWS // SCALE_ROWS,),
        in_specs=smem() + [pl.BlockSpec((SCALE_ROWS, TOK), lambda g: (g, 0))],
        out_specs=pl.BlockSpec((SCALE_ROWS, TOK), lambda g: (g, 0)),
        out_shape=shape((ROWS, TOK), F32),
        compiler_params=PARAMS,
        name="scale",
    )(factor, value)


def dscore_kernel(me_ref, ret_ref, *refs):
    late_refs = refs[:NDP]
    out_ref = refs[NDP]
    owner_id = lax.broadcasted_iota(jnp.int32, (OWN, TOK), 0)
    place_id = lax.broadcasted_iota(jnp.int32, (CAP, TOK), 0)
    row = lax.broadcasted_iota(jnp.int32, (PICKS, TOK), 0)
    for s in range(NDP):
        late_ref = late_refs[s]
        which = source(me_ref[0], s)
        square = jnp.concatenate([ret_ref[:, which, :]] * 4, axis=0)
        columns = jnp.transpose(square)[0:CAP, 0:OWN]
        stacked = jnp.concatenate(pieces(columns), axis=0)
        target = [late_index(late_ref, k, 3) for k in range(PICKS)]
        chosen = jnp.concatenate(
            [
                jnp.where(owner_id == jnp.right_shift(target[k], 7), 1.0, 0.0).astype(BF16)
                for k in range(PICKS)
            ],
            axis=1,
        )
        got = lax.dot_general(stacked, chosen, NN, preferred_element_type=F32)
        got = (got[0:CAP, :] + got[CAP : 2 * CAP, :]) + got[2 * CAP : 3 * CAP, :]
        picked = jnp.concatenate(
            [
                jnp.sum(
                    jnp.where(
                        place_id == jnp.bitwise_and(target[k], TOK - 1),
                        got[:, k * TOK : (k + 1) * TOK],
                        0.0,
                    ),
                    axis=0,
                    keepdims=True,
                )
                for k in range(PICKS)
            ],
            axis=0,
        )
        weight = jnp.concatenate(
            [
                joined(*[late_ref[p : p + 1, k * TOK : (k + 1) * TOK] for p in range(3)])
                for k in range(PICKS)
            ],
            axis=0,
        )
        both = weight * picked
        mean0 = jnp.sum(both[0:4, :], axis=0, keepdims=True)
        mean1 = jnp.sum(both[4:8, :], axis=0, keepdims=True)
        at = pl.multiple_of(which * 8, 8)
        slope = weight * (picked - jnp.where(row < 4, mean0, mean1))
        for d in range(NDP):
            out_ref[d, pl.ds(at, 8), :] = slope


def partial_dscore(me, returned, late):
    return pl.pallas_call(
        dscore_kernel,
        grid=(1,),
        in_specs=smem()
        + vmem(1)
        + [pl.BlockSpec((EXTRA, 4 * HALF), lambda g: (TOK // EXTRA, 0))] * NDP,
        out_specs=vmem(1)[0],
        out_shape=shape((NDP, NDP * PICKS, TOK), F32),
        compiler_params=PARAMS,
        name="dscore",
    )(me, returned, *late)


def key_kernel(me_ref, ds_ref, *refs):
    late_refs = refs[:NDP]
    out_ref = refs[NDP]
    base = me_ref[0] * KEYS
    dscore = []
    for s in range(NDP):
        at = pl.multiple_of(source(me_ref[0], s) * 8, 8)
        total = ds_ref[0, pl.ds(at, 8), :]
        for d in range(1, NDP):
            total = total + ds_ref[d, pl.ds(at, 8), :]
        dscore.append(total)
    key_id = lax.broadcasted_iota(jnp.int32, (KEYS, TOK), 0) + base
    for half in range(2):
        for head in range(2):
            at = head * 2 * HALF + half * HALF
            blocks = []
            for s in range(NDP):
                block = jnp.zeros((KEYS, TOK), F32)
                for k in range(4):
                    slot = head * 4 + k
                    value = dscore[s][slot : slot + 1, :]
                    block = block + jnp.where(
                        key_id == late_index(late_refs[s], slot, TOK + 5 + 2 * half), value, 0.0
                    )
                blocks.append(block)
            weighted = jnp.concatenate(blocks, axis=1)
            query = jnp.concatenate(
                [late_refs[s][0:TOK, at : at + HALF] for s in range(NDP)], axis=0
            )
            stacked = jnp.concatenate(pieces(weighted), axis=0)
            total = lax.dot_general(stacked, query, NN, preferred_element_type=F32)
            total = (total[0:KEYS, :] + total[KEYS : 2 * KEYS, :]) + total[2 * KEYS : 3 * KEYS, :]
            r = half * 4 + head * 2
            out_ref[:, r : r + 2, :] = total.reshape(OWN, 2, HALF)


def key_terms(me, dscore, late):
    return pl.pallas_call(
        key_kernel,
        in_specs=smem() + vmem(1 + NDP),
        out_specs=vmem(1)[0],
        out_shape=shape((OWN, 8, HALF), F32),
        compiler_params=PARAMS,
        name="key_terms",
    )(me, dscore, *late)


def exchange(x, axis):
    return lax.all_to_all(x, axis, 0, 0, tiled=True)


def everyone(x, axis, size):
    return exchange(jnp.broadcast_to(x[None], (size, *x.shape)), axis)


def body(queries, sub_keys, values, slot_first, slot_second, cotangent):
    q = queries.reshape(TOK, 4 * HALF)
    first = slot_first.reshape(TOK, PICKS).T
    second = slot_second.reshape(TOK, PICKS).T
    me = lax.axis_index("dp").astype(jnp.int32).reshape(1)
    outgoing, late = prep(q, sub_keys, first, second, cotangent)
    sent = exchange(outgoing, "dp")
    expanded = expand(0, sent)
    rows_a = exchange(expanded, TABLE)
    expanded = expand(1, sent)
    rows_b = exchange(expanded, TABLE)
    late, _ = lax.optimization_barrier((late, sent))
    late_all = [late] + [
        lax.ppermute(late, "dp", [(i, (i + k) % NDP) for i in range(NDP)])
        for k in range(1, NDP)
    ]
    row, weight = decode(rows_a)
    value_rows = gather_rows(row, values.reshape(ROWS, TOK))
    partial = dots(0, rows_a, value_rows)
    partial = dots(1, rows_b, value_rows, (partial,))
    returned = exchange(partial.reshape(OWN, NDP, TOK), TABLE)
    value_grad, value_sq = scatter_rows(row, weight, rows_a, rows_b)
    slopes = partial_dscore(me, returned, late_all)
    dscore = exchange(slopes, "dp")
    key_grad = key_terms(me, dscore, late_all)
    key_pieces = exchange(key_grad, TABLE)
    key_part = jnp.sum(key_pieces, axis=0)
    local_sq = (jnp.sum(value_sq) + jnp.sum(key_part * key_part)).reshape(1)
    chip_sq = local_sq + lax.ppermute(local_sq, "table_2", [(0, 1), (1, 0)])
    total_sq = jnp.sum(everyone(chip_sq, CHIPS, OWN * NDP // 2))
    clip_factor = jnp.minimum(
        1.0, LIMIT_RATIO * math.sqrt(TOK * OWN * NDP) / jnp.sqrt(total_sq)
    ).reshape(1)
    value_update = scaled(clip_factor, value_grad).reshape(BLK, NSUB, TOK)
    key_update = (clip_factor[0] * key_part).reshape(2, 2, 2, HALF)
    return (value_update, key_update, clip_factor)


def solution(mesh):
    torus = Mesh(
        mesh.devices.reshape(mesh.shape["dp"], 4, 4, 2), ("dp", "table_0", "table_1", "table_2")
    )
    return jax.shard_map(
        body,
        mesh=torus,
        in_specs=(
            P(DP_TABLE, None, None),
            P(),
            P(TABLE, None, "dp"),
            P(DP_TABLE, None, None),
            P(DP_TABLE, None, None),
            P(DP_TABLE, None),
        ),
        out_specs=(P(TABLE, None, "dp"), P(None, None, DP_TABLE, None), P()),
        check_vma=False,
    )
```

profile of v0, /device:TPU:1, one launch (start us, length us, event | category | flops | bytes accessed | tf_op | source)
XLA Modules:
  0.0 226.9 jit_solution(6932006848610881722)
XLA Ops:
  0.6 1.0 copy.11
  1.6 1.2 copy-done.8
  2.8 0.9 copy-done.12
  5.2 1.2 prep.1
  6.4 22.4 %all_to_all.36.sent_ref = bf16[8,192,128]{2,1,0:T(8,128)(2,1)S(1)} all-to-all(bf16[8,192,128]{2,1,0:T(8,128)(2,1)S(1)} %get-tuple-element.10), channel_id=1, replica_groups=mesh['dp'=8,'table_0'=4,'table_1'=4,'table_2'=2] {'dp'}, dimensions={0} | all-to-all | bytes 786432 | tf_op jit(solution)/shard_map/all_to_all | solution.py:562
  28.8 2.6 %expand.2 = bf16[32,208,128]{2,1,0:T(8,128)(2,1)} custom-call(bf16[8,192,128]{2,1,0:T(8,128)(2,1)S(1)} %all_to_all.36.sent_ref), custom_call_target="tpu_custom_call" | custom-call | tf_op jit(solution)/shard_map/expand/pallas_call | solution.py:217
  31.4 9.1 %all-to-all-start.1 = ((bf16[32,208,128]{2,1,0:T(8,128)(2,1)}), bf16[32,208,128]{2,1,0:T(8,128)(2,1)S(1)}, u32[]{:S(2)}, u32[]{:S(2)}) async-start(bf16[32,208,128]{2,1,0:T(8,128)(2,1)} %expand.2), calls=%async_computation.1 | async-start | bytes 3407872 | tf_op jit(solution)/shard_map/all_to_all | solution.py:562
  40.6 2.5 %expand.3 = bf16[32,192,128]{2,1,0:T(8,128)(2,1)} custom-call(bf16[8,192,128]{2,1,0:T(8,128)(2,1)S(1)} %all_to_all.36.sent_ref), custom_call_target="tpu_custom_call" | custom-call | tf_op jit(solution)/shard_map/expand/pallas_call | solution.py:217
  43.1 22.1 %all-to-all-done.1.rows_ref.rows_a_ref.refs_0_ = bf16[32,208,128]{2,1,0:T(8,128)(2,1)S(1)} async-done(((bf16[32,208,128]{2,1,0:T(8,128)(2,1)}), bf16[32,208,128]{2,1,0:T(8,128)(2,1)S(1)}, u32[]{:S(2)}, u32[]{:S(2)}) %all-to-all-start.1) | async-done | bytes 1703968 | tf_op jit(solution)/shard_map/all_to_all | solution.py:562
  65.1 5.5 %all-to-all-start.2 = ((bf16[32,192,128]{2,1,0:T(8,128)(2,1)}), bf16[32,192,128]{2,1,0:T(8,128)(2,1)}, u32[]{:S(2)}, u32[]{:S(2)}) async-start(bf16[32,192,128]{2,1,0:T(8,128)(2,1)} %expand.3), calls=%async_computation.2 | async-start | bytes 3145728 | tf_op jit(solution)/shard_map/all_to_all | solution.py:562
  71.1 2.0 collective-permute-start.2
  73.1 3.4 %collective-permute-start.3 = (bf16[144,1024]{1,0:T(8,128)(2,1)S(1)}, bf16[144,1024]{1,0:T(8,128)(2,1)}, u32[]{:S(2)}, u32[]{:S(2)}) collective-permute-start(bf16[144,1024]{1,0:T(8,128)(2,1)S(1)} %get-tuple-element.15.refs_0_), channel_id=1, source_target_pairs={{0,128},{32,160},{64,192},{96,224},{128,0},{160,32},{192,64},{224,... | collective-permute-start | bytes 884744 | tf_op jit(solution)/shard_map/ppermute | solution.py:582
  77.4 6.4 %collective-permute-done.refs_1_ = bf16[144,1024]{1,0:T(8,128)(2,1)S(1)} collective-permute-done((bf16[144,1024]{1,0:T(8,128)(2,1)S(1)}, bf16[144,1024]{1,0:T(8,128)(2,1)S(1)}, u32[]{:S(2)}, u32[]{:S(2)}) %collective-permute-start) | collective-permute-done | bytes 294944 | tf_op jit(solution)/shard_map/ppermute | solution.py:582
  83.8 2.4 %collective-permute-done.1.refs_2_ = bf16[144,1024]{1,0:T(8,128)(2,1)S(1)} collective-permute-done((bf16[144,1024]{1,0:T(8,128)(2,1)S(1)}, bf16[144,1024]{1,0:T(8,128)(2,1)S(1)}, u32[]{:S(2)}, u32[]{:S(2)}) %collective-permute-start.1) | collective-permute-done | bytes 294944 | tf_op jit(solution)/shard_map/ppermute | solution.py:582
  86.2 10.4 %collective-permute-start.6 = (bf16[144,1024]{1,0:T(8,128)(2,1)S(1)}, bf16[144,1024]{1,0:T(8,128)(2,1)}, u32[]{:S(2)}, u32[]{:S(2)}) collective-permute-start(bf16[144,1024]{1,0:T(8,128)(2,1)S(1)} %get-tuple-element.15.refs_0_), channel_id=1, source_target_pairs={{0,224},{32,0},{64,32},{96,64},{128,96},{160,128},{192,160},{224,1... | collective-permute-start | bytes 884744 | tf_op jit(solution)/shard_map/ppermute | solution.py:582
  97.3 1.6 copy-done.3
  99.0 16.4 %gather_rows.1.refs_1_ = bf16[12288,128]{1,0:T(8,128)(2,1)S(1)} custom-call(s32[256,128]{1,0:T(8,128)S(1)} %get-tuple-element.11.row_ref, bf16[8192,128]{1,0:T(8,128)(2,1)S(1)} %bitcast.15), custom_call_target="tpu_custom_call" | custom-call | tf_op jit(solution)/shard_map/gather_rows/pallas_call | solution.py:280
  115.4 1.2 dots.2.refs_2_
  116.6 2.9 %dots.3 = f32[256,128]{1,0:T(8,128)S(1)} custom-call(bf16[32,192,128]{2,1,0:T(8,128)(2,1)} %all-to-all-done.2.rows_b_ref.refs_0_, bf16[12288,128]{1,0:T(8,128)(2,1)S(1)} %gather_rows.1.refs_1_, f32[128,128]{1,0:T(8,128)S(1)} %dots.2.refs_2_), custom_call_target="tpu_custom_call" | custom-call | tf_op jit(solution)/shard_map/dots/pallas_call | solution.py:321
  120.2 11.1 %all-to-all-start.3 = ((f32[32,8,128]{2,1,0:T(8,128)}), f32[32,8,128]{2,1,0:T(8,128)S(1)}, u32[]{:S(2)}, u32[]{:S(2)}) async-start(f32[32,8,128]{2,1,0:T(8,128)} %bitcast.17), calls=%async_computation.3 | async-start | bytes 262144 | tf_op jit(solution)/shard_map/all_to_all | solution.py:562
  131.4 7.5 %all-to-all-done.3.ret_ref = f32[32,8,128]{2,1,0:T(8,128)S(1)} async-done(((f32[32,8,128]{2,1,0:T(8,128)}), f32[32,8,128]{2,1,0:T(8,128)S(1)}, u32[]{:S(2)}, u32[]{:S(2)}) %all-to-all-start.3) | async-done | bytes 131104 | tf_op jit(solution)/shard_map/all_to_all | solution.py:562
  139.0 1.0 copy-done.5
  139.9 1.0 copy-done.7
  140.9 1.7 dscore.1
  142.6 16.3 %all_to_all.37.ds_ref = f32[8,64,128]{2,1,0:T(8,128)S(1)} all-to-all(f32[8,64,128]{2,1,0:T(8,128)S(1)} %dscore.1), channel_id=1, replica_groups=mesh['dp'=8,'table_0'=4,'table_1'=4,'table_2'=2] {'dp'}, dimensions={0} | all-to-all | bytes 524288 | tf_op jit(solution)/shard_map/all_to_all | solution.py:562
  158.9 3.1 %key_terms.1 = f32[32,8,256]{2,1,0:T(8,128)} custom-call(s32[1]{0:T(128)} %bitcast.4.me_ref, f32[8,64,128]{2,1,0:T(8,128)S(1)} %all_to_all.37.ds_ref, bf16[144,1024]{1,0:T(8,128)(2,1)S(1)} %get-tuple-element.15.refs_0_, bf16[144,1024]{1,0:T(8,128)(2,1)S(1)} %copy-done.5, bf16[144,1024]{1,0:T(8,128)(2,1)S(1)} %copy-done.7, ...), custom_call_target="tpu_custom_call" | custom-call | tf_op jit(solution)/shard_map/key_terms/pallas_call | solution.py:551
  162.1 5.4 %all-to-all-start.5 = ((f32[32,8,256]{2,1,0:T(8,128)}), f32[32,8,256]{2,1,0:T(8,128)S(1)}, u32[]{:S(2)}, u32[]{:S(2)}) async-start(f32[32,8,256]{2,1,0:T(8,128)} %key_terms.1), calls=%async_computation.5 | async-start | bytes 524288 | tf_op jit(solution)/shard_map/all_to_all | solution.py:562
  167.4 26.5 %scatter_rows.1 = (f32[8192,128]{1,0:T(8,128)}, f32[8,128]{1,0:T(8,128)S(1)}) custom-call(s32[256,128]{1,0:T(8,128)S(1)} %copy-done.11, f32[256,128]{1,0:T(8,128)S(1)} %copy-done.14, bf16[32,208,128]{2,1,0:T(8,128)(2,1)} %copy-done, bf16[32,192,128]{2,1,0:T(8,128)(2,1)} %all-to-all-done.2.rows_b_ref.refs_0_), custom_call_target="tpu_custom_call" | custom-call | tf_op jit(solution)/shard_map/scatter_rows/pallas_call | solution.py:405
  196.5 1.4 collective-permute-start.7
  198.6 19.5 %all_to_all.38 = f32[128,1,1]{2,1,0:T(1,128)S(1)} all-to-all(f32[128,1,1]{2,1,0:T(1,128)S(1)} %broadcast_in_dim.9), channel_id=1, replica_groups=mesh['dp'=8,'table_0'=4,'table_1'=4,'table_2'=2] {'dp','table_0','table_1'}, dimensions={0} | all-to-all | bytes 1024 | tf_op jit(solution)/shard_map/all_to_all | solution.py:562
  220.1 2.2 copy-done.2
  222.3 3.5 %scale.1 = f32[8192,128]{1,0:T(8,128)} custom-call(f32[1]{0:T(128)} %bitcast.9.factor_ref, f32[8192,128]{1,0:T(8,128)S(1)} %copy-done.2), custom_call_target="tpu_custom_call" | custom-call | tf_op jit(solution)/shard_map/scale/pallas_call | solution.py:436
  (48 shorter events, 6.8 us)
Async XLA Ops:
  1.6 1.2 copy-start.8
  2.8 0.9 copy-start.12
  3.8 0.7 copy-start.15
  4.5 0.7 copy-start.16
  31.4 33.7 %all-to-all-start.1 = ((bf16[32,208,128]{2,1,0:T(8,128)(2,1)}), bf16[32,208,128]{2,1,0:T(8,128)(2,1)S(1)}, u32[]{:S(2)}, u32[]{:S(2)}) async-start(bf16[32,208,128]{2,1,0:T(8,128)(2,1)} %expand.2), calls=%async_computation.1 | async-start | bytes 3407872 | tf_op jit(solution)/shard_map/all_to_all | solution.py:562
  65.1 31.5 %copy-start = (bf16[32,208,128]{2,1,0:T(8,128)(2,1)}, bf16[32,208,128]{2,1,0:T(8,128)(2,1)S(1)}, u32[]{:S(2)}) copy-start(bf16[32,208,128]{2,1,0:T(8,128)(2,1)S(1)} %all-to-all-done.1.rows_ref.rows_a_ref.refs_0_) | copy-start | bytes 5111812
  65.1 51.5 %all-to-all-start.2 = ((bf16[32,192,128]{2,1,0:T(8,128)(2,1)}), bf16[32,192,128]{2,1,0:T(8,128)(2,1)}, u32[]{:S(2)}, u32[]{:S(2)}) async-start(bf16[32,192,128]{2,1,0:T(8,128)(2,1)} %expand.3), calls=%async_computation.2 | async-start | bytes 3145728 | tf_op jit(solution)/shard_map/all_to_all | solution.py:562
  70.6 13.1 %collective-permute-start = (bf16[144,1024]{1,0:T(8,128)(2,1)S(1)}, bf16[144,1024]{1,0:T(8,128)(2,1)S(1)}, u32[]{:S(2)}, u32[]{:S(2)}) collective-permute-start(bf16[144,1024]{1,0:T(8,128)(2,1)S(1)} %get-tuple-element.15.refs_0_), channel_id=1, source_target_pairs={{0,32},{32,64},{64,96},{96,128},{128,160},{160,192},{192,224},{224... | collective-permute-start | bytes 884744 | tf_op jit(solution)/shard_map/ppermute | solution.py:582
  71.0 15.2 %collective-permute-start.1 = (bf16[144,1024]{1,0:T(8,128)(2,1)S(1)}, bf16[144,1024]{1,0:T(8,128)(2,1)S(1)}, u32[]{:S(2)}, u32[]{:S(2)}) collective-permute-start(bf16[144,1024]{1,0:T(8,128)(2,1)S(1)} %get-tuple-element.15.refs_0_), channel_id=1, source_target_pairs={{0,64},{32,96},{64,128},{96,160},{128,192},{160,224},{192,0},{224,... | collective-permute-start | bytes 884744 | tf_op jit(solution)/shard_map/ppermute | solution.py:582
  71.1 60.3 %collective-permute-start.2 = (bf16[144,1024]{1,0:T(8,128)(2,1)S(1)}, bf16[144,1024]{1,0:T(8,128)(2,1)}, u32[]{:S(2)}, u32[]{:S(2)}) collective-permute-start(bf16[144,1024]{1,0:T(8,128)(2,1)S(1)} %get-tuple-element.15.refs_0_), channel_id=1, source_target_pairs={{0,96},{32,128},{64,160},{96,192},{128,224},{160,0},{192,32},{224,... | collective-permute-start | bytes 884744 | tf_op jit(solution)/shard_map/ppermute | solution.py:582
  73.1 58.3 %collective-permute-start.3 = (bf16[144,1024]{1,0:T(8,128)(2,1)S(1)}, bf16[144,1024]{1,0:T(8,128)(2,1)}, u32[]{:S(2)}, u32[]{:S(2)}) collective-permute-start(bf16[144,1024]{1,0:T(8,128)(2,1)S(1)} %get-tuple-element.15.refs_0_), channel_id=1, source_target_pairs={{0,128},{32,160},{64,192},{96,224},{128,0},{160,32},{192,64},{224,... | collective-permute-start | bytes 884744 | tf_op jit(solution)/shard_map/ppermute | solution.py:582
  76.5 55.0 %collective-permute-start.4 = (bf16[144,1024]{1,0:T(8,128)(2,1)S(1)}, bf16[144,1024]{1,0:T(8,128)(2,1)}, u32[]{:S(2)}, u32[]{:S(2)}) collective-permute-start(bf16[144,1024]{1,0:T(8,128)(2,1)S(1)} %get-tuple-element.15.refs_0_), channel_id=1, source_target_pairs={{0,160},{32,192},{64,224},{96,0},{128,32},{160,64},{192,96},{224,1... | collective-permute-start | bytes 884744 | tf_op jit(solution)/shard_map/ppermute | solution.py:582
  83.8 13.6 %copy-start.4 = (bf16[144,1024]{1,0:T(8,128)(2,1)}, bf16[144,1024]{1,0:T(8,128)(2,1)S(1)}, u32[]{:S(2)}) copy-start(bf16[144,1024]{1,0:T(8,128)(2,1)S(1)} %collective-permute-done.refs_1_) | copy-start | bytes 884740
  83.8 47.7 %collective-permute-start.5 = (bf16[144,1024]{1,0:T(8,128)(2,1)S(1)}, bf16[144,1024]{1,0:T(8,128)(2,1)}, u32[]{:S(2)}, u32[]{:S(2)}) collective-permute-start(bf16[144,1024]{1,0:T(8,128)(2,1)S(1)} %get-tuple-element.15.refs_0_), channel_id=1, source_target_pairs={{0,192},{32,224},{64,0},{96,32},{128,64},{160,96},{192,128},{224,1... | collective-permute-start | bytes 884744 | tf_op jit(solution)/shard_map/ppermute | solution.py:582
  86.2 11.1 %copy-start.6 = (bf16[144,1024]{1,0:T(8,128)(2,1)}, bf16[144,1024]{1,0:T(8,128)(2,1)S(1)}, u32[]{:S(2)}) copy-start(bf16[144,1024]{1,0:T(8,128)(2,1)S(1)} %collective-permute-done.1.refs_2_) | copy-start | bytes 884740
  86.2 45.3 %collective-permute-start.6 = (bf16[144,1024]{1,0:T(8,128)(2,1)S(1)}, bf16[144,1024]{1,0:T(8,128)(2,1)}, u32[]{:S(2)}, u32[]{:S(2)}) collective-permute-start(bf16[144,1024]{1,0:T(8,128)(2,1)S(1)} %get-tuple-element.15.refs_0_), channel_id=1, source_target_pairs={{0,224},{32,0},{64,32},{96,64},{128,96},{160,128},{192,160},{224,1... | collective-permute-start | bytes 884744 | tf_op jit(solution)/shard_map/ppermute | solution.py:582
  96.7 0.6 copy-start.13
  97.3 18.1 %copy-start.10 = (s32[256,128]{1,0:T(8,128)}, s32[256,128]{1,0:T(8,128)S(1)}, u32[]{:S(2)}) copy-start(s32[256,128]{1,0:T(8,128)S(1)} %get-tuple-element.11.row_ref) | copy-start | bytes 393220
  97.3 1.6 copy-start.3
  98.9 16.4 %copy-start.1 = (bf16[32,208,128]{2,1,0:T(8,128)(2,1)S(1)}, bf16[32,208,128]{2,1,0:T(8,128)(2,1)}, u32[]{:S(2)}) copy-start(bf16[32,208,128]{2,1,0:T(8,128)(2,1)} %copy-done) | copy-start | bytes 5111812
  119.6 0.7 copy-start.9
  120.2 18.7 %all-to-all-start.3 = ((f32[32,8,128]{2,1,0:T(8,128)}), f32[32,8,128]{2,1,0:T(8,128)S(1)}, u32[]{:S(2)}, u32[]{:S(2)}) async-start(f32[32,8,128]{2,1,0:T(8,128)} %bitcast.17), calls=%async_computation.3 | async-start | bytes 262144 | tf_op jit(solution)/shard_map/all_to_all | solution.py:562
  139.0 1.0 copy-start.5
  139.9 1.0 copy-start.7
  142.6 24.8 %copy-start.11 = (s32[256,128]{1,0:T(8,128)S(1)}, s32[256,128]{1,0:T(8,128)}, u32[]{:S(2)}) copy-start(s32[256,128]{1,0:T(8,128)} %copy-done.10) | copy-start | bytes 393220
  142.6 24.8 %copy-start.14 = (f32[256,128]{1,0:T(8,128)S(1)}, f32[256,128]{1,0:T(8,128)}, u32[]{:S(2)}) copy-start(f32[256,128]{1,0:T(8,128)} %copy-done.13) | copy-start | bytes 393220
  162.1 32.5 %all-to-all-start.5 = ((f32[32,8,256]{2,1,0:T(8,128)}), f32[32,8,256]{2,1,0:T(8,128)S(1)}, u32[]{:S(2)}, u32[]{:S(2)}) async-start(f32[32,8,256]{2,1,0:T(8,128)} %key_terms.1), calls=%async_computation.5 | async-start | bytes 524288 | tf_op jit(solution)/shard_map/all_to_all | solution.py:562
  196.5 1.4 collective-permute-start.7
  220.1 2.2 copy-start.2
where the time goes:
time: 228 us; the launch traced here: 227 us
  Pallas kernels  61.9 us (27%)
  blocking collectives  58.2 us (26%)
  starting transfers between devices  49.6 us (22%)
  waiting for transfers between devices  38.4 us (17%)
  local copies, waits for them, and re-layouts  12.2 us (5%)
  between operations  4.64 us (2%)
    all_to_all x3, blocking collectives, exchange(): return lax.all_to_all(x, axis, 0, 0, tiled=True)  58.2 us
    all_to_all x4, starting transfers between devices, exchange(): return lax.all_to_all(x, axis, 0, 0, tiled=True)  31.1 us
    all_to_all x4, waiting for transfers between devices, exchange(): return lax.all_to_all(x, axis, 0, 0, tiled=True)  29.6 us
    pallas_call x1, Pallas kernels, scatter_rows(): pl.pallas_call(scatter_kernel, grid=(2 * SCATTER_STEPS,), in_specs=smem()...  26.5 us
    ppermute x7, starting transfers between devices, body(): lax.ppermute(late, 'dp', [(i, (i + k) % NDP) for i in range(NDP)])  17.1 us
    pallas_call x1, Pallas kernels, gather_rows(): pl.pallas_call(gather_kernel, grid=(LISTS // GATHER_LISTS,), in_specs=sme...  16.4 us
    unnamed x35, local copies, waits for them, and re-layouts  11.6 us
    ppermute x7, waiting for transfers between devices, body(): lax.ppermute(late, 'dp', [(i, (i + k) % NDP) for i in range(NDP)])  8.8 us
  transfers between devices with their start and end apart: 12, of which 4 were waited for; matrix products, arithmetic and copies ran while one was open for 0% of the time, Pallas kernels for 22%

commit v1 on v0

--- a/solution.py
+++ b/solution.py
@@ -24,7 +24,6 @@
 KEYS = NSUB // NDP
 LISTS = OWN * NDP
 PART = NDP // 2
-PART_LISTS = OWN * PART
 ROWS = BLK * NSUB
 RECORDS = 2 * NDP
 ACCS = 8
@@ -228,10 +227,12 @@
 def decode_kernel(rows_ref, row_ref, weight_ref, wide_ref):
     for t in range(OWN):
         wide_ref[t * RECORDS : (t + 1) * RECORDS, :] = rows_ref[t, PART * CAP :, :].astype(F32)
-    index = wide_ref[pl.ds(0, LISTS, stride=2), :]
-    weight = wide_ref[pl.ds(1, LISTS, stride=2), :]
-    row_ref[...] = (index * 32.0 + pltpu.roll(index, TOK - CAP, 1)).astype(jnp.int32)
-    weight_ref[...] = weight + pltpu.roll(weight, TOK - CAP, 1)
+    for s in range(NDP):
+        index = wide_ref[pl.ds(2 * s, OWN, stride=RECORDS), :]
+        weight = wide_ref[pl.ds(2 * s + 1, OWN, stride=RECORDS), :]
+        at = slice(s * OWN, (s + 1) * OWN)
+        row_ref[at, :] = (index * 32.0 + pltpu.roll(index, TOK - CAP, 1)).astype(jnp.int32)
+        weight_ref[at, :] = weight + pltpu.roll(weight, TOK - CAP, 1)
 
 
 def decode(rows):
@@ -246,13 +247,8 @@
     )(rows)
 
 
-GATHER_LISTS = 32
-
-
 def gather_kernel(row_ref, table_ref, out_ref, wide_ref, got_ref):
-    step = pl.program_id(0)
-
-    @pl.when(step == 0)
+    @pl.when(pl.program_id(0) == 0)
     def _():
         def widen(i, carry):
             at = pl.multiple_of(i * 256, 256)
@@ -261,31 +257,26 @@
 
         lax.fori_loop(0, ROWS // 256, widen, 0)
 
-    part = step // (PART_LISTS // GATHER_LISTS)
-    first_list = (step % (PART_LISTS // GATHER_LISTS)) * GATHER_LISTS
-
-    def one_list(i, carry):
-        at = first_list + i
-        which = (at // PART) * NDP + part * PART + at % PART
+    for t in range(OWN):
         for j in range(CAP):
-            row = row_ref[which, j]
-            got_ref[pl.ds(i * CAP + j, 1), :] = wide_ref[pl.ds(row, 1), :]
-        return carry
-
-    lax.fori_loop(0, GATHER_LISTS, one_list, 0)
-    out_ref[...] = got_ref[...].astype(BF16)
+            row = row_ref[t, j]
+            got_ref[pl.ds(t * CAP + j, 1), :] = wide_ref[pl.ds(row, 1), :]
+    out_ref[...] = got_ref[...].astype(BF16).reshape(1, OWN, CAP, TOK)
 
 
 def gather_rows(row, table):
     return pl.pallas_call(
         gather_kernel,
-        grid=(LISTS // GATHER_LISTS,),
-        in_specs=smem() + [pl.BlockSpec((ROWS, TOK), lambda g: (0, 0))],
-        out_specs=pl.BlockSpec((GATHER_LISTS * CAP, TOK), lambda g: (g, 0)),
-        out_shape=shape((LISTS * CAP, TOK), BF16),
+        grid=(NDP,),
+        in_specs=[
+            pl.BlockSpec((OWN, TOK), lambda g: (g, 0), memory_space=pltpu.SMEM),
+            pl.BlockSpec((ROWS, TOK), lambda g: (0, 0)),
+        ],
+        out_specs=pl.BlockSpec((1, OWN, CAP, TOK), lambda g: (g, 0, 0, 0)),
+        out_shape=shape((NDP, OWN, CAP, TOK), BF16),
         scratch_shapes=[
             pltpu.VMEM((ROWS, TOK), F32),
-            pltpu.VMEM((GATHER_LISTS * CAP, TOK), F32),
+            pltpu.VMEM((OWN * CAP, TOK), F32),
         ],
         compiler_params=PARAMS,
         name="gather_rows",
@@ -306,9 +297,8 @@
         if part == 1:
             made.append(refs[2][t * PART : (t + 1) * PART, :])
         for k in range(PART):
-            at = (t * PART + k) * CAP
             product = rows_ref[t, k * CAP : (k + 1) * CAP, :].astype(F32) * value_ref[
-                at : at + CAP, :
+                k, t
             ].astype(F32)
             total = jnp.sum(product, axis=1, keepdims=True)
             made.append(jnp.sum(jnp.where(own, total, 0.0), axis=0, keepdims=True))
@@ -323,7 +313,7 @@
         grid=(steps,),
         in_specs=[
             pl.BlockSpec((DOT_OWN, rows.shape[1], TOK), lambda g: (g, 0, 0)),
-            pl.BlockSpec((DOT_OWN * PART * CAP, TOK), lambda g: (part * steps + g, 0)),
+            pl.BlockSpec((PART, DOT_OWN, CAP, TOK), lambda g: (part, g, 0, 0)),
         ]
         + [pl.BlockSpec((DOT_OWN * PART, TOK), lambda g: (g, 0))] * len(earlier),
         out_specs=pl.BlockSpec((count, TOK), lambda g: (g, 0)),
@@ -331,10 +321,6 @@
         compiler_params=PARAMS,
         name="dots",
     )(rows, value, *earlier)
-
-
-SCATTER_OWN = 8
-SCATTER_STEPS = OWN // SCATTER_OWN
 
 
 def scatter_kernel(row_ref, weight_ref, rows_a_ref, rows_b_ref, out_ref, sq_ref, wide_ref, *accs):
@@ -350,41 +336,29 @@
 
         lax.fori_loop(0, ROWS // 64, clear, 0)
 
-    block = step % SCATTER_STEPS
-    part = step // SCATTER_STEPS
-    at = pl.multiple_of(block * SCATTER_OWN * NDP, SCATTER_OWN * NDP)
-    weight = weight_ref[pl.ds(at, SCATTER_OWN * NDP), :]
-    columns = jnp.transpose(jnp.concatenate([weight] * (TOK // (SCATTER_OWN * NDP)), axis=0))
-    for which, rows_ref in ((0, rows_a_ref), (1, rows_b_ref)):
-
-        @pl.when(part == which)
+    columns = jnp.transpose(jnp.concatenate([weight_ref[...]] * (TOK // OWN), axis=0))
+    for part, rows_ref in ((0, rows_a_ref), (1, rows_b_ref)):
+
+        @pl.when(step // PART == part)
         def _():
-            for t in range(SCATTER_OWN):
-                for k in range(PART):
-                    i = t * PART + k
-                    s = t * NDP + which * PART + k
-                    wide_ref[i * CAP : (i + 1) * CAP, :] = (
-                        rows_ref[t, k * CAP : (k + 1) * CAP, :].astype(F32)
-                        * columns[0:CAP, s : s + 1]
-                    )
-
-    def one_list(i, carry):
-        which = (block * SCATTER_OWN + i // PART) * NDP + part * PART + i % PART
-        waiting = []
+            for t in range(OWN):
+                wide_ref[t * CAP : (t + 1) * CAP, :] = (
+                    rows_ref[t].astype(F32) * columns[0:CAP, t : t + 1]
+                )
+
+    waiting = []
+    for t in range(OWN):
         for b in range(0, CAP, BATCH):
             made = []
             for j in range(b, b + BATCH):
                 acc = accs[j % ACCS]
-                row = row_ref[which, j]
-                made.append((acc, row, acc[pl.ds(row, 1), :] + wide_ref[pl.ds(i * CAP + j, 1), :]))
+                row = row_ref[t, j]
+                made.append((acc, row, acc[pl.ds(row, 1), :] + wide_ref[pl.ds(t * CAP + j, 1), :]))
             for acc, row, total in waiting:
                 acc[pl.ds(row, 1), :] = total
             waiting = made
-        for acc, row, total in waiting:
-            acc[pl.ds(row, 1), :] = total
-        return carry
-
-    lax.fori_loop(0, SCATTER_OWN * PART, one_list, 0)
+    for acc, row, total in waiting:
+        acc[pl.ds(row, 1), :] = total
 
     @pl.when(step == pl.num_programs(0) - 1)
     def _():
@@ -401,24 +375,18 @@
 
 
 def scatter_rows(row, weight, rows_a, rows_b):
-    last = SCATTER_STEPS - 1
     return pl.pallas_call(
         scatter_kernel,
-        grid=(2 * SCATTER_STEPS,),
-        in_specs=smem()
-        + vmem(1)
-        + [
-            pl.BlockSpec(
-                (SCATTER_OWN, rows_a.shape[1], TOK), lambda g: (jnp.minimum(g, last), 0, 0)
-            ),
-            pl.BlockSpec(
-                (SCATTER_OWN, rows_b.shape[1], TOK),
-                lambda g: (jnp.maximum(g - SCATTER_STEPS, 0), 0, 0),
-            ),
+        grid=(NDP,),
+        in_specs=[
+            pl.BlockSpec((OWN, TOK), lambda g: (g, 0), memory_space=pltpu.SMEM),
+            pl.BlockSpec((OWN, TOK), lambda g: (g, 0)),
+            pl.BlockSpec((OWN, CAP, TOK), lambda g: (0, jnp.minimum(g, PART - 1), 0)),
+            pl.BlockSpec((OWN, CAP, TOK), lambda g: (0, jnp.maximum(g - PART, 0), 0)),
         ],
         out_specs=vmem(2),
         out_shape=(shape((ROWS, TOK), F32), shape((8, TOK), F32)),
-        scratch_shapes=[pltpu.VMEM((SCATTER_OWN * PART * CAP, TOK), F32)]
+        scratch_shapes=[pltpu.VMEM((OWN * CAP, TOK), F32)]
         + [pltpu.VMEM((ROWS, TOK), F32) for _ in range(ACCS)],
         compiler_params=pltpu.CompilerParams(vmem_limit_bytes=52 * 1024 * 1024),
         name="scatter_rows",
@@ -439,7 +407,7 @@
         in_specs=smem() + [pl.BlockSpec((SCALE_ROWS, TOK), lambda g: (g, 0))],
         out_specs=pl.BlockSpec((SCALE_ROWS, TOK), lambda g: (g, 0)),
         out_shape=shape((ROWS, TOK), F32),
-        compiler_params=PARAMS,
+        compiler_params=pltpu.CompilerParams(vmem_limit_bytes=60 * 1024 * 1024),
         name="scale",
     )(factor, value)
 

time: 228 us -> 220 us (0.965)
  Pallas kernels: 61.9 us -> 55.7 us
    pallas_call x2, Pallas kernels: 43 us -> 33.5 us  [the longest x1 22.3 us: scatter_rows(): pl.pallas_call(scatter_kernel, grid=(NDP,), in_specs=[pl.BlockSpec((OWN,...]
    pallas_call x1, Pallas kernels: 3.48 us -> 6.59 us  [scaled(): pl.pallas_call(scale_kernel, grid=(ROWS // SCALE_ROWS,), in_specs=smem()...]
    unnamed x35 -> x33, local copies, waits for them, and re-layouts: 11.6 us -> 9.38 us
  transfers between devices with their start and end apart: 12 -> 12, of which waited for: 4 -> 5; matrix products, arithmetic and copies ran while one was open for 0% -> 0% of each run, Pallas kernels for 22% -> 19%
where the time goes in v1:
time: 220 us; the launch traced here: 219 us
  blocking collectives  58.3 us (26%)
  Pallas kernels  55.7 us (25%)
  starting transfers between devices  49.6 us (23%)
  waiting for transfers between devices  38.4 us (17%)
  local copies, waits for them, and re-layouts  10 us (5%)
  between operations  4.56 us (2%)
    all_to_all x3, blocking collectives, exchange(): return lax.all_to_all(x, axis, 0, 0, tiled=True)  58.3 us
    all_to_all x4, starting transfers between devices, exchange(): return lax.all_to_all(x, axis, 0, 0, tiled=True)  31.1 us
    all_to_all x4, waiting for transfers between devices, exchange(): return lax.all_to_all(x, axis, 0, 0, tiled=True)  28.5 us
    pallas_call x1, Pallas kernels, scatter_rows(): pl.pallas_call(scatter_kernel, grid=(NDP,), in_specs=[pl.BlockSpec((OWN,...  22.3 us
    ppermute x7, starting transfers between devices, body(): lax.ppermute(late, 'dp', [(i, (i + k) % NDP) for i in range(NDP)])  17.1 us
    pallas_call x1, Pallas kernels, gather_rows(): pl.pallas_call(gather_kernel, grid=(NDP,), in_specs=[pl.BlockSpec((OWN, T...  11.2 us
    ppermute x7, waiting for transfers between devices, body(): lax.ppermute(late, 'dp', [(i, (i + k) % NDP) for i in range(NDP)])  9.92 us
    unnamed x33, local copies, waits for them, and re-layouts  9.38 us
  transfers between devices with their start and end apart: 12, of which 5 were waited for; matrix products, arithmetic and copies ran while one was open for 0% of the time, Pallas kernels for 19%

profile of v1, /device:TPU:1, one launch (start us, length us, event | category | flops | bytes accessed | tf_op | source)
XLA Modules:
  0.0 218.6 jit_solution(16059806847855454413)
XLA Ops:
  0.6 1.0 copy.11
  1.6 1.2 copy-done.7
  2.8 0.9 copy-done.11
  5.2 1.2 prep.1
  6.4 22.4 %all_to_all.36.sent_ref = bf16[8,192,128]{2,1,0:T(8,128)(2,1)S(1)} all-to-all(bf16[8,192,128]{2,1,0:T(8,128)(2,1)S(1)} %get-tuple-element.10), channel_id=1, replica_groups=mesh['dp'=8,'table_0'=4,'table_1'=4,'table_2'=2] {'dp'}, dimensions={0} | all-to-all | bytes 786432 | tf_op jit(solution)/shard_map/all_to_all | solution.py:530
  28.8 2.6 %expand.2 = bf16[32,208,128]{2,1,0:T(8,128)(2,1)} custom-call(bf16[8,192,128]{2,1,0:T(8,128)(2,1)S(1)} %all_to_all.36.sent_ref), custom_call_target="tpu_custom_call" | custom-call | tf_op jit(solution)/shard_map/expand/pallas_call | solution.py:216
  31.4 9.1 %all-to-all-start.1 = ((bf16[32,208,128]{2,1,0:T(8,128)(2,1)}), bf16[32,208,128]{2,1,0:T(8,128)(2,1)S(1)}, u32[]{:S(2)}, u32[]{:S(2)}) async-start(bf16[32,208,128]{2,1,0:T(8,128)(2,1)} %expand.2), calls=%async_computation.1 | async-start | bytes 3407872 | tf_op jit(solution)/shard_map/all_to_all | solution.py:530
  40.6 2.5 %expand.3 = bf16[32,192,128]{2,1,0:T(8,128)(2,1)} custom-call(bf16[8,192,128]{2,1,0:T(8,128)(2,1)S(1)} %all_to_all.36.sent_ref), custom_call_target="tpu_custom_call" | custom-call | tf_op jit(solution)/shard_map/expand/pallas_call | solution.py:216
  43.1 22.1 %all-to-all-done.1.rows_ref.rows_a_ref.refs_0_ = bf16[32,208,128]{2,1,0:T(8,128)(2,1)S(1)} async-done(((bf16[32,208,128]{2,1,0:T(8,128)(2,1)}), bf16[32,208,128]{2,1,0:T(8,128)(2,1)S(1)}, u32[]{:S(2)}, u32[]{:S(2)}) %all-to-all-start.1) | async-done | bytes 1703968 | tf_op jit(solution)/shard_map/all_to_all | solution.py:530
  65.1 5.5 %all-to-all-start.2 = ((bf16[32,192,128]{2,1,0:T(8,128)(2,1)}), bf16[32,192,128]{2,1,0:T(8,128)(2,1)}, u32[]{:S(2)}, u32[]{:S(2)}) async-start(bf16[32,192,128]{2,1,0:T(8,128)(2,1)} %expand.3), calls=%async_computation.2 | async-start | bytes 3145728 | tf_op jit(solution)/shard_map/all_to_all | solution.py:530
  71.1 2.0 collective-permute-start.2
  73.1 3.4 %collective-permute-start.3 = (bf16[144,1024]{1,0:T(8,128)(2,1)S(1)}, bf16[144,1024]{1,0:T(8,128)(2,1)}, u32[]{:S(2)}, u32[]{:S(2)}) collective-permute-start(bf16[144,1024]{1,0:T(8,128)(2,1)S(1)} %get-tuple-element.15.refs_0_), channel_id=1, source_target_pairs={{0,128},{32,160},{64,192},{96,224},{128,0},{160,32},{192,64},{224,... | collective-permute-start | bytes 884744 | tf_op jit(solution)/shard_map/ppermute | solution.py:550
  77.4 6.4 %collective-permute-done.refs_1_ = bf16[144,1024]{1,0:T(8,128)(2,1)S(1)} collective-permute-done((bf16[144,1024]{1,0:T(8,128)(2,1)S(1)}, bf16[144,1024]{1,0:T(8,128)(2,1)S(1)}, u32[]{:S(2)}, u32[]{:S(2)}) %collective-permute-start) | collective-permute-done | bytes 294944 | tf_op jit(solution)/shard_map/ppermute | solution.py:550
  83.8 2.4 %collective-permute-done.1.refs_2_ = bf16[144,1024]{1,0:T(8,128)(2,1)S(1)} collective-permute-done((bf16[144,1024]{1,0:T(8,128)(2,1)S(1)}, bf16[144,1024]{1,0:T(8,128)(2,1)S(1)}, u32[]{:S(2)}, u32[]{:S(2)}) %collective-permute-start.1) | collective-permute-done | bytes 294944 | tf_op jit(solution)/shard_map/ppermute | solution.py:550
  86.2 10.4 %collective-permute-start.6 = (bf16[144,1024]{1,0:T(8,128)(2,1)S(1)}, bf16[144,1024]{1,0:T(8,128)(2,1)}, u32[]{:S(2)}, u32[]{:S(2)}) collective-permute-start(bf16[144,1024]{1,0:T(8,128)(2,1)S(1)} %get-tuple-element.15.refs_0_), channel_id=1, source_target_pairs={{0,224},{32,0},{64,32},{96,64},{128,96},{160,128},{192,160},{224,1... | collective-permute-start | bytes 884744 | tf_op jit(solution)/shard_map/ppermute | solution.py:550
  97.4 1.6 copy-done.2
  99.0 11.2 %gather_rows.1.refs_1_ = bf16[8,32,48,128]{3,2,1,0:T(8,128)(2,1)S(1)} custom-call(s32[256,128]{1,0:T(8,128)S(1)} %get-tuple-element.11.row_ref, bf16[8192,128]{1,0:T(8,128)(2,1)S(1)} %bitcast.15), custom_call_target="tpu_custom_call" | custom-call | tf_op jit(solution)/shard_map/gather_rows/pallas_call | solution.py:268
  110.3 1.3 dots.2.refs_2_
  111.6 3.0 %dots.3 = f32[256,128]{1,0:T(8,128)S(1)} custom-call(bf16[32,192,128]{2,1,0:T(8,128)(2,1)} %all-to-all-done.2.rows_b_ref.refs_0_, bf16[8,32,48,128]{3,2,1,0:T(8,128)(2,1)S(1)} %gather_rows.1.refs_1_, f32[128,128]{1,0:T(8,128)S(1)} %dots.2.refs_2_), custom_call_target="tpu_custom_call" | custom-call | tf_op jit(solution)/shard_map/dots/pallas_call | solution.py:311
  115.2 11.1 %all-to-all-start.3 = ((f32[32,8,128]{2,1,0:T(8,128)}), f32[32,8,128]{2,1,0:T(8,128)S(1)}, u32[]{:S(2)}, u32[]{:S(2)}) async-start(f32[32,8,128]{2,1,0:T(8,128)} %bitcast.17), calls=%async_computation.3 | async-start | bytes 262144 | tf_op jit(solution)/shard_map/all_to_all | solution.py:530
  126.4 1.1 collective-permute-done.6.refs_7_
  127.5 6.4 %all-to-all-done.3.ret_ref = f32[32,8,128]{2,1,0:T(8,128)S(1)} async-done(((f32[32,8,128]{2,1,0:T(8,128)}), f32[32,8,128]{2,1,0:T(8,128)S(1)}, u32[]{:S(2)}, u32[]{:S(2)}) %all-to-all-start.3) | async-done | bytes 131104 | tf_op jit(solution)/shard_map/all_to_all | solution.py:530
  134.0 1.0 copy-done.4
  134.9 1.0 copy-done.6
  135.9 1.7 dscore.1
  137.6 16.3 %all_to_all.37.ds_ref = f32[8,64,128]{2,1,0:T(8,128)S(1)} all-to-all(f32[8,64,128]{2,1,0:T(8,128)S(1)} %dscore.1), channel_id=1, replica_groups=mesh['dp'=8,'table_0'=4,'table_1'=4,'table_2'=2] {'dp'}, dimensions={0} | all-to-all | bytes 524288 | tf_op jit(solution)/shard_map/all_to_all | solution.py:530
  154.0 3.1 %key_terms.1 = f32[32,8,256]{2,1,0:T(8,128)} custom-call(s32[1]{0:T(128)} %bitcast.4.me_ref, f32[8,64,128]{2,1,0:T(8,128)S(1)} %all_to_all.37.ds_ref, bf16[144,1024]{1,0:T(8,128)(2,1)S(1)} %get-tuple-element.15.refs_0_, bf16[144,1024]{1,0:T(8,128)(2,1)S(1)} %copy-done.4, bf16[144,1024]{1,0:T(8,128)(2,1)S(1)} %copy-done.6, ...), custom_call_target="tpu_custom_call" | custom-call | tf_op jit(solution)/shard_map/key_terms/pallas_call | solution.py:519
  157.1 5.3 %all-to-all-start.5 = ((f32[32,8,256]{2,1,0:T(8,128)}), f32[32,8,256]{2,1,0:T(8,128)S(1)}, u32[]{:S(2)}, u32[]{:S(2)}) async-start(f32[32,8,256]{2,1,0:T(8,128)} %key_terms.1), calls=%async_computation.5 | async-start | bytes 524288 | tf_op jit(solution)/shard_map/all_to_all | solution.py:530
  162.4 22.3 %scatter_rows.1 = (f32[8192,128]{1,0:T(8,128)}, f32[8,128]{1,0:T(8,128)S(1)}) custom-call(s32[256,128]{1,0:T(8,128)S(1)} %copy-done.10, f32[256,128]{1,0:T(8,128)S(1)} %copy-done.13, bf16[32,208,128]{2,1,0:T(8,128)(2,1)} %copy-done, bf16[32,192,128]{2,1,0:T(8,128)(2,1)} %all-to-all-done.2.rows_b_ref.refs_0_), custom_call_target="tpu_custom_call" | custom-call | tf_op jit(solution)/shard_map/scatter_rows/pallas_call | solution.py:378
  187.3 1.4 collective-permute-start.7
  189.2 19.6 %all_to_all.38 = f32[128,1,1]{2,1,0:T(1,128)S(1)} all-to-all(f32[128,1,1]{2,1,0:T(1,128)S(1)} %broadcast_in_dim.9), channel_id=1, replica_groups=mesh['dp'=8,'table_0'=4,'table_1'=4,'table_2'=2] {'dp','table_0','table_1'}, dimensions={0} | all-to-all | bytes 1024 | tf_op jit(solution)/shard_map/all_to_all | solution.py:530
  210.8 6.6 %scale.1 = f32[8192,128]{1,0:T(8,128)} custom-call(f32[1]{0:T(128)} %bitcast.9.factor_ref, f32[8192,128]{1,0:T(8,128)} %get-tuple-element.16.value_ref), custom_call_target="tpu_custom_call" | custom-call | tf_op jit(solution)/shard_map/scale/pallas_call | solution.py:404
  (46 shorter events, 6.9 us)
Async XLA Ops:
  1.6 1.2 copy-start.7
  2.8 0.9 copy-start.11
  3.8 0.7 copy-start.14
  4.5 0.7 copy-start.15
  31.4 33.7 %all-to-all-start.1 = ((bf16[32,208,128]{2,1,0:T(8,128)(2,1)}), bf16[32,208,128]{2,1,0:T(8,128)(2,1)S(1)}, u32[]{:S(2)}, u32[]{:S(2)}) async-start(bf16[32,208,128]{2,1,0:T(8,128)(2,1)} %expand.2), calls=%async_computation.1 | async-start | bytes 3407872 | tf_op jit(solution)/shard_map/all_to_all | solution.py:530
  65.1 31.6 %copy-start = (bf16[32,208,128]{2,1,0:T(8,128)(2,1)}, bf16[32,208,128]{2,1,0:T(8,128)(2,1)S(1)}, u32[]{:S(2)}) copy-start(bf16[32,208,128]{2,1,0:T(8,128)(2,1)S(1)} %all-to-all-done.1.rows_ref.rows_a_ref.refs_0_) | copy-start | bytes 5111812
  65.1 46.5 %all-to-all-start.2 = ((bf16[32,192,128]{2,1,0:T(8,128)(2,1)}), bf16[32,192,128]{2,1,0:T(8,128)(2,1)}, u32[]{:S(2)}, u32[]{:S(2)}) async-start(bf16[32,192,128]{2,1,0:T(8,128)(2,1)} %expand.3), calls=%async_computation.2 | async-start | bytes 3145728 | tf_op jit(solution)/shard_map/all_to_all | solution.py:530
  70.6 13.1 %collective-permute-start = (bf16[144,1024]{1,0:T(8,128)(2,1)S(1)}, bf16[144,1024]{1,0:T(8,128)(2,1)S(1)}, u32[]{:S(2)}, u32[]{:S(2)}) collective-permute-start(bf16[144,1024]{1,0:T(8,128)(2,1)S(1)} %get-tuple-element.15.refs_0_), channel_id=1, source_target_pairs={{0,32},{32,64},{64,96},{96,128},{128,160},{160,192},{192,224},{224... | collective-permute-start | bytes 884744 | tf_op jit(solution)/shard_map/ppermute | solution.py:550
  71.0 15.2 %collective-permute-start.1 = (bf16[144,1024]{1,0:T(8,128)(2,1)S(1)}, bf16[144,1024]{1,0:T(8,128)(2,1)S(1)}, u32[]{:S(2)}, u32[]{:S(2)}) collective-permute-start(bf16[144,1024]{1,0:T(8,128)(2,1)S(1)} %get-tuple-element.15.refs_0_), channel_id=1, source_target_pairs={{0,64},{32,96},{64,128},{96,160},{128,192},{160,224},{192,0},{224,... | collective-permute-start | bytes 884744 | tf_op jit(solution)/shard_map/ppermute | solution.py:550
  71.1 55.3 %collective-permute-start.2 = (bf16[144,1024]{1,0:T(8,128)(2,1)S(1)}, bf16[144,1024]{1,0:T(8,128)(2,1)}, u32[]{:S(2)}, u32[]{:S(2)}) collective-permute-start(bf16[144,1024]{1,0:T(8,128)(2,1)S(1)} %get-tuple-element.15.refs_0_), channel_id=1, source_target_pairs={{0,96},{32,128},{64,160},{96,192},{128,224},{160,0},{192,32},{224,... | collective-permute-start | bytes 884744 | tf_op jit(solution)/shard_map/ppermute | solution.py:550
  73.1 53.3 %collective-permute-start.3 = (bf16[144,1024]{1,0:T(8,128)(2,1)S(1)}, bf16[144,1024]{1,0:T(8,128)(2,1)}, u32[]{:S(2)}, u32[]{:S(2)}) collective-permute-start(bf16[144,1024]{1,0:T(8,128)(2,1)S(1)} %get-tuple-element.15.refs_0_), channel_id=1, source_target_pairs={{0,128},{32,160},{64,192},{96,224},{128,0},{160,32},{192,64},{224,... | collective-permute-start | bytes 884744 | tf_op jit(solution)/shard_map/ppermute | solution.py:550
  76.5 49.9 %collective-permute-start.4 = (bf16[144,1024]{1,0:T(8,128)(2,1)S(1)}, bf16[144,1024]{1,0:T(8,128)(2,1)}, u32[]{:S(2)}, u32[]{:S(2)}) collective-permute-start(bf16[144,1024]{1,0:T(8,128)(2,1)S(1)} %get-tuple-element.15.refs_0_), channel_id=1, source_target_pairs={{0,160},{32,192},{64,224},{96,0},{128,32},{160,64},{192,96},{224,1... | collective-permute-start | bytes 884744 | tf_op jit(solution)/shard_map/ppermute | solution.py:550
  83.8 13.6 %copy-start.3 = (bf16[144,1024]{1,0:T(8,128)(2,1)}, bf16[144,1024]{1,0:T(8,128)(2,1)S(1)}, u32[]{:S(2)}) copy-start(bf16[144,1024]{1,0:T(8,128)(2,1)S(1)} %collective-permute-done.refs_1_) | copy-start | bytes 884740
  83.8 42.7 %collective-permute-start.5 = (bf16[144,1024]{1,0:T(8,128)(2,1)S(1)}, bf16[144,1024]{1,0:T(8,128)(2,1)}, u32[]{:S(2)}, u32[]{:S(2)}) collective-permute-start(bf16[144,1024]{1,0:T(8,128)(2,1)S(1)} %get-tuple-element.15.refs_0_), channel_id=1, source_target_pairs={{0,192},{32,224},{64,0},{96,32},{128,64},{160,96},{192,128},{224,1... | collective-permute-start | bytes 884744 | tf_op jit(solution)/shard_map/ppermute | solution.py:550
  86.2 11.2 %copy-start.5 = (bf16[144,1024]{1,0:T(8,128)(2,1)}, bf16[144,1024]{1,0:T(8,128)(2,1)S(1)}, u32[]{:S(2)}) copy-start(bf16[144,1024]{1,0:T(8,128)(2,1)S(1)} %collective-permute-done.1.refs_2_) | copy-start | bytes 884740
  86.2 41.4 %collective-permute-start.6 = (bf16[144,1024]{1,0:T(8,128)(2,1)S(1)}, bf16[144,1024]{1,0:T(8,128)(2,1)}, u32[]{:S(2)}, u32[]{:S(2)}) collective-permute-start(bf16[144,1024]{1,0:T(8,128)(2,1)S(1)} %get-tuple-element.15.refs_0_), channel_id=1, source_target_pairs={{0,224},{32,0},{64,32},{96,64},{128,96},{160,128},{192,160},{224,1... | collective-permute-start | bytes 884744 | tf_op jit(solution)/shard_map/ppermute | solution.py:550
  96.7 0.7 copy-start.12
  97.4 12.9 %copy-start.9 = (s32[256,128]{1,0:T(8,128)}, s32[256,128]{1,0:T(8,128)S(1)}, u32[]{:S(2)}) copy-start(s32[256,128]{1,0:T(8,128)S(1)} %get-tuple-element.11.row_ref) | copy-start | bytes 393220
  97.4 1.6 copy-start.2
  99.0 11.2 %copy-start.1 = (bf16[32,208,128]{2,1,0:T(8,128)(2,1)S(1)}, bf16[32,208,128]{2,1,0:T(8,128)(2,1)}, u32[]{:S(2)}) copy-start(bf16[32,208,128]{2,1,0:T(8,128)(2,1)} %copy-done) | copy-start | bytes 5111812
  114.6 0.6 copy-start.8
  115.2 18.7 %all-to-all-start.3 = ((f32[32,8,128]{2,1,0:T(8,128)}), f32[32,8,128]{2,1,0:T(8,128)S(1)}, u32[]{:S(2)}, u32[]{:S(2)}) async-start(f32[32,8,128]{2,1,0:T(8,128)} %bitcast.17), calls=%async_computation.3 | async-start | bytes 262144 | tf_op jit(solution)/shard_map/all_to_all | solution.py:530
  134.0 1.0 copy-start.4
  134.9 1.0 copy-start.6
  137.6 24.8 %copy-start.10 = (s32[256,128]{1,0:T(8,128)S(1)}, s32[256,128]{1,0:T(8,128)}, u32[]{:S(2)}) copy-start(s32[256,128]{1,0:T(8,128)} %copy-done.9) | copy-start | bytes 393220
  137.6 24.8 %copy-start.13 = (f32[256,128]{1,0:T(8,128)S(1)}, f32[256,128]{1,0:T(8,128)}, u32[]{:S(2)}) copy-start(f32[256,128]{1,0:T(8,128)} %copy-done.12) | copy-start | bytes 393220
  157.1 28.2 %all-to-all-start.5 = ((f32[32,8,256]{2,1,0:T(8,128)}), f32[32,8,256]{2,1,0:T(8,128)S(1)}, u32[]{:S(2)}, u32[]{:S(2)}) async-start(f32[32,8,256]{2,1,0:T(8,128)} %key_terms.1), calls=%async_computation.5 | async-start | bytes 524288 | tf_op jit(solution)/shard_map/all_to_all | solution.py:530
  187.3 1.4 collective-permute-start.7

commit v2 on v1

--- a/solution.py
+++ b/solution.py
@@ -37,6 +37,7 @@
 NN = (((1,), (0,)), ((), ()))
 
 PARAMS = pltpu.CompilerParams(vmem_limit_bytes=20 * 1024 * 1024)
+WIDE_PARAMS = pltpu.CompilerParams(vmem_limit_bytes=52 * 1024 * 1024)
 
 
 def pieces(x):
@@ -164,7 +165,7 @@
             shape((NDP, TOK + 2 * OWN, TOK), BF16),
             shape((TOK + EXTRA, 4 * HALF), BF16),
         ),
-        compiler_params=PARAMS,
+        compiler_params=WIDE_PARAMS,
         name="prep",
     )(q, keys, first, second, cot)
 
@@ -318,12 +319,38 @@
         + [pl.BlockSpec((DOT_OWN * PART, TOK), lambda g: (g, 0))] * len(earlier),
         out_specs=pl.BlockSpec((count, TOK), lambda g: (g, 0)),
         out_shape=shape((count * steps, TOK), F32),
-        compiler_params=PARAMS,
+        compiler_params=PARAMS if part == 0 else WIDE_PARAMS,
         name="dots",
     )(rows, value, *earlier)
 
 
-def scatter_kernel(row_ref, weight_ref, rows_a_ref, rows_b_ref, out_ref, sq_ref, wide_ref, *accs):
+def weigh_kernel(weight_ref, rows_ref, *refs):
+    out_ref = refs[-1]
+    columns = jnp.transpose(jnp.concatenate([weight_ref[...]] * (TOK // OWN), axis=0))
+    for t in range(OWN):
+        out_ref[t * CAP : (t + 1) * CAP, :] = (
+            rows_ref[t].astype(F32) * columns[0:CAP, t : t + 1]
+        )
+
+
+def weigh(part, weight, rows, earlier=()):
+    return pl.pallas_call(
+        weigh_kernel,
+        grid=(PART,),
+        in_specs=[
+            pl.BlockSpec((OWN, TOK), lambda g: (part * PART + g, 0)),
+            pl.BlockSpec((OWN, CAP, TOK), lambda g: (0, g, 0)),
+        ]
+        + [pl.BlockSpec(memory_space=pl.ANY)] * len(earlier),
+        out_specs=pl.BlockSpec((OWN * CAP, TOK), lambda g: (part * PART + g, 0)),
+        out_shape=shape((LISTS * CAP, TOK), F32),
+        input_output_aliases={2: 0} if earlier else {},
+        compiler_params=WIDE_PARAMS,
+        name="weigh",
+    )(weight, rows, *earlier)
+
+
+def scatter_kernel(row_ref, wide_ref, out_ref, sq_ref, *accs):
     step = pl.program_id(0)
 
     @pl.when(step == 0)
@@ -335,16 +362,6 @@
             return carry
 
         lax.fori_loop(0, ROWS // 64, clear, 0)
-
-    columns = jnp.transpose(jnp.concatenate([weight_ref[...]] * (TOK // OWN), axis=0))
-    for part, rows_ref in ((0, rows_a_ref), (1, rows_b_ref)):
-
-        @pl.when(step // PART == part)
-        def _():
-            for t in range(OWN):
-                wide_ref[t * CAP : (t + 1) * CAP, :] = (
-                    rows_ref[t].astype(F32) * columns[0:CAP, t : t + 1]
-                )
 
     waiting = []
     for t in range(OWN):
@@ -374,42 +391,98 @@
         sq_ref[...] = lax.fori_loop(0, ROWS // 64, collect, jnp.zeros((8, TOK), F32))
 
 
-def scatter_rows(row, weight, rows_a, rows_b):
+def scatter_rows(row, wide):
     return pl.pallas_call(
         scatter_kernel,
         grid=(NDP,),
         in_specs=[
             pl.BlockSpec((OWN, TOK), lambda g: (g, 0), memory_space=pltpu.SMEM),
-            pl.BlockSpec((OWN, TOK), lambda g: (g, 0)),
-            pl.BlockSpec((OWN, CAP, TOK), lambda g: (0, jnp.minimum(g, PART - 1), 0)),
-            pl.BlockSpec((OWN, CAP, TOK), lambda g: (0, jnp.maximum(g - PART, 0), 0)),
+            pl.BlockSpec((OWN * CAP, TOK), lambda g: (g, 0)),
         ],
         out_specs=vmem(2),
         out_shape=(shape((ROWS, TOK), F32), shape((8, TOK), F32)),
-        scratch_shapes=[pltpu.VMEM((OWN * CAP, TOK), F32)]
-        + [pltpu.VMEM((ROWS, TOK), F32) for _ in range(ACCS)],
-        compiler_params=pltpu.CompilerParams(vmem_limit_bytes=52 * 1024 * 1024),
+        scratch_shapes=[pltpu.VMEM((ROWS, TOK), F32) for _ in range(ACCS)],
+        compiler_params=WIDE_PARAMS,
         name="scatter_rows",
-    )(row, weight, rows_a, rows_b)
-
-
-SCALE_ROWS = 1024
-
-
-def scale_kernel(factor_ref, value_ref, out_ref):
-    out_ref[...] = value_ref[...] * factor_ref[0]
-
-
-def scaled(factor, value):
-    return pl.pallas_call(
-        scale_kernel,
-        grid=(ROWS // SCALE_ROWS,),
-        in_specs=smem() + [pl.BlockSpec((SCALE_ROWS, TOK), lambda g: (g, 0))],
-        out_specs=pl.BlockSpec((SCALE_ROWS, TOK), lambda g: (g, 0)),
-        out_shape=shape((ROWS, TOK), F32),
-        compiler_params=pltpu.CompilerParams(vmem_limit_bytes=60 * 1024 * 1024),
+    )(row, wide)
+
+
+def finish_kernel(pieces_ref, sq_ref, part_ref, local_ref):
+    part = pieces_ref[0]
+    for t in range(1, OWN):
+        part = part + pieces_ref[t]
+    part_ref[...] = part
+    square = part * part
+    total = sq_ref[...] + (square[:, 0:TOK] + square[:, TOK:])
+    total = jnp.sum(jnp.sum(total, axis=0, keepdims=True), axis=1, keepdims=True)
+    local_ref[...] = jnp.broadcast_to(total, (1, TOK))
+
+
+def finish(key_pieces, value_sq):
+    return pl.pallas_call(
+        finish_kernel,
+        in_specs=vmem(2),
+        out_specs=vmem(2),
+        out_shape=(shape((8, HALF), F32), shape((1, TOK), F32)),
+        compiler_params=PARAMS,
+        name="finish",
+    )(key_pieces, value_sq)
+
+
+CHUNKS = 8
+
+
+def scale_kernel(limit, sums_ref, part_ref, value_ref, out_ref, key_ref, clip_ref, buf, come, go):
+    size = ROWS // CHUNKS
+
+    def part_of(ref, i):
+        return ref.at[pl.ds(i * size, size), :]
+
+    reads = [
+        pltpu.make_async_copy(part_of(value_ref, i), part_of(buf, i), come.at[i])
+        for i in range(CHUNKS)
+    ]
+    writes = [
+        pltpu.make_async_copy(part_of(buf, i), part_of(out_ref, i), go.at[i])
+        for i in range(CHUNKS)
+    ]
+    for read in reads:
+        read.start()
+    total = jnp.sum(sums_ref[...], axis=0, keepdims=True)
+    factor = jnp.minimum(1.0, limit / jnp.sqrt(total))
+    clip_ref[...] = factor
+    keys = part_ref[...] * jnp.concatenate([factor, factor], axis=1)
+    for half in range(2):
+        for head in range(2):
+            r = half * 4 + head * 2
+            key_ref[half, head] = keys[r : r + 2, :]
+    for i in range(CHUNKS):
+        reads[i].wait()
+        at = slice(i * size, (i + 1) * size)
+        buf[at, :] = buf[at, :] * factor
+        writes[i].start()
+    for write in writes:
+        write.wait()
+
+
+def scaled(limit, sums, key_part, value):
+    return pl.pallas_call(
+        functools.partial(scale_kernel, limit),
+        in_specs=vmem(2) + [pl.BlockSpec(memory_space=pl.ANY)],
+        out_specs=[pl.BlockSpec(memory_space=pl.ANY)] + vmem(2),
+        out_shape=(
+            shape((ROWS, TOK), F32),
+            shape((2, 2, 2, HALF), F32),
+            shape((1, TOK), F32),
+        ),
+        scratch_shapes=[
+            pltpu.VMEM((ROWS, TOK), F32),
+            pltpu.SemaphoreType.DMA((CHUNKS,)),
+            pltpu.SemaphoreType.DMA((CHUNKS,)),
+        ],
+        compiler_params=WIDE_PARAMS,
         name="scale",
-    )(factor, value)
+    )(sums, key_part, value)
 
 
 def dscore_kernel(me_ref, ret_ref, *refs):
@@ -555,21 +628,25 @@
     partial = dots(0, rows_a, value_rows)
     partial = dots(1, rows_b, value_rows, (partial,))
     returned = exchange(partial.reshape(OWN, NDP, TOK), TABLE)
-    value_grad, value_sq = scatter_rows(row, weight, rows_a, rows_b)
+    wide = weigh(0, weight, rows_a)
+    wide = weigh(1, weight, rows_b, (wide,))
+    value_grad, value_sq = scatter_rows(row, wide)
     slopes = partial_dscore(me, returned, late_all)
     dscore = exchange(slopes, "dp")
     key_grad = key_terms(me, dscore, late_all)
     key_pieces = exchange(key_grad, TABLE)
-    key_part = jnp.sum(key_pieces, axis=0)
-    local_sq = (jnp.sum(value_sq) + jnp.sum(key_part * key_part)).reshape(1)
+    key_part, local_sq = finish(key_pieces, value_sq)
     chip_sq = local_sq + lax.ppermute(local_sq, "table_2", [(0, 1), (1, 0)])
-    total_sq = jnp.sum(everyone(chip_sq, CHIPS, OWN * NDP // 2))
-    clip_factor = jnp.minimum(
-        1.0, LIMIT_RATIO * math.sqrt(TOK * OWN * NDP) / jnp.sqrt(total_sq)
-    ).reshape(1)
-    value_update = scaled(clip_factor, value_grad).reshape(BLK, NSUB, TOK)
-    key_update = (clip_factor[0] * key_part).reshape(2, 2, 2, HALF)
-    return (value_update, key_update, clip_factor)
+    sums = everyone(chip_sq, CHIPS, OWN * NDP // 2)
+    limit = LIMIT_RATIO * math.sqrt(TOK * OWN * NDP)
+    value_update, key_update, clip = scaled(
+        limit, sums.reshape(OWN * NDP // 2, TOK), key_part, value_grad
+    )
+    return (
+        value_update.reshape(BLK, NSUB, TOK),
+        key_update,
+        clip[0, 0:1],
+    )
 
 
 def solution(mesh):

time: 220 us -> 214 us (0.973)
  starting transfers between devices: 49.6 us -> 40.4 us
  waiting for transfers between devices: 38.4 us -> 43.8 us
  Pallas kernels: 55.7 us -> 59.8 us
  between operations: 4.56 us -> 1.02 us
    ppermute x7, waiting for transfers between devices: 9.92 us -> 18.8 us  [body(): lax.ppermute(late, 'dp', [(i, (i + k) % NDP) for i in range(NDP)])]
    ppermute x7, starting transfers between devices: 17.1 us -> 9.19 us  [body(): lax.ppermute(late, 'dp', [(i, (i + k) % NDP) for i in range(NDP)])]
    pallas_call x1 -> x4, Pallas kernels: 6.59 us -> 12.4 us  [the longest x2 8.1 us: weigh(): pl.pallas_call(weigh_kernel, grid=(PART,), in_specs=[pl.BlockSpec((OWN, T...]
    all_to_all x4, waiting for transfers between devices: 28.5 us -> 24.2 us  [exchange(): return lax.all_to_all(x, axis, 0, 0, tiled=True)]
    pallas_call x1, Pallas kernels: 22.3 us -> 18.9 us  [scatter_rows(): pl.pallas_call(scatter_kernel, grid=(NDP,), in_specs=[pl.BlockSpec((OWN,...]
    unnamed x33 -> x35, local copies, waits for them, and re-layouts: 9.38 us -> 8.48 us
  transfers between devices with their start and end apart: 12 -> 12, of which waited for: 5 -> 6; matrix products, arithmetic and copies ran while one was open for 0% -> 0% of each run, Pallas kernels for 19% -> 21%
where the time goes in v2:
time: 214 us; the launch traced here: 213 us
  Pallas kernels  59.8 us (28%)
  blocking collectives  59.8 us (28%)
  waiting for transfers between devices  43.8 us (20%)
  starting transfers between devices  40.4 us (19%)
  local copies, waits for them, and re-layouts  8.51 us (4%)
    all_to_all x3, blocking collectives, exchange(): return lax.all_to_all(x, axis, 0, 0, tiled=True)  59.8 us
    all_to_all x4, starting transfers between devices, exchange(): return lax.all_to_all(x, axis, 0, 0, tiled=True)  30.9 us
    all_to_all x4, waiting for transfers between devices, exchange(): return lax.all_to_all(x, axis, 0, 0, tiled=True)  24.2 us
    pallas_call x1, Pallas kernels, scatter_rows(): pl.pallas_call(scatter_kernel, grid=(NDP,), in_specs=[pl.BlockSpec((OWN,...  18.9 us
    ppermute x7, waiting for transfers between devices, body(): lax.ppermute(late, 'dp', [(i, (i + k) % NDP) for i in range(NDP)])  18.8 us
    pallas_call x1, Pallas kernels, gather_rows(): pl.pallas_call(gather_kernel, grid=(NDP,), in_specs=[pl.BlockSpec((OWN, T...  11.2 us
    ppermute x7, starting transfers between devices, body(): lax.ppermute(late, 'dp', [(i, (i + k) % NDP) for i in range(NDP)])  9.19 us
    unnamed x35, local copies, waits for them, and re-layouts  8.48 us
  transfers between devices with their start and end apart: 12, of which 6 were waited for; matrix products, arithmetic and copies ran while one was open for 0% of the time, Pallas kernels for 21%

profile of v2, /device:TPU:1, one launch (start us, length us, event | category | flops | bytes accessed | tf_op | source)
XLA Modules:
  0.0 213.3 jit_solution(6926106299210445015)
XLA Ops:
  0.6 1.0 copy.10
  1.6 0.9 copy-done.14
  3.9 2.5 %prep.1 = (bf16[8,192,128]{2,1,0:T(8,128)(2,1)S(1)}, bf16[144,1024]{1,0:T(8,128)(2,1)S(1)}) custom-call(bf16[128,1024]{1,0:T(8,128)(2,1)S(1)} %bitcast.18, bf16[2,2,512,256]{3,2,1,0:T(8,128)(2,1)} %keys_ref.1, s32[8,128]{1,0:T(8,128)S(1)} %bitcast.21, s32[8,128]{1,0:T(8,128)S(1)} %bitcast.22, bf16[128,1024]{1,0:T(8,128)(2,1)S(1)} %copy-done.14), custom_call_target="tpu_custom_call" | custom-call | tf_op jit(solution)/shard_map/prep/pallas_call | solution.py:160
  6.5 22.4 %all_to_all.35.sent_ref = bf16[8,192,128]{2,1,0:T(8,128)(2,1)S(1)} all-to-all(bf16[8,192,128]{2,1,0:T(8,128)(2,1)S(1)} %get-tuple-element.15), channel_id=1, replica_groups=mesh['dp'=8,'table_0'=4,'table_1'=4,'table_2'=2] {'dp'}, dimensions={0} | all-to-all | bytes 786432 | tf_op jit(solution)/shard_map/all_to_all | solution.py:603
  28.8 2.6 %expand.3 = bf16[32,208,128]{2,1,0:T(8,128)(2,1)} custom-call(bf16[8,192,128]{2,1,0:T(8,128)(2,1)S(1)} %all_to_all.35.sent_ref), custom_call_target="tpu_custom_call" | custom-call | tf_op jit(solution)/shard_map/expand/pallas_call | solution.py:217
  31.4 9.2 %all-to-all-start.2 = ((bf16[32,208,128]{2,1,0:T(8,128)(2,1)}), bf16[32,208,128]{2,1,0:T(8,128)(2,1)S(1)}, u32[]{:S(2)}, u32[]{:S(2)}) async-start(bf16[32,208,128]{2,1,0:T(8,128)(2,1)} %expand.3), calls=%async_computation.2 | async-start | bytes 3407872 | tf_op jit(solution)/shard_map/all_to_all | solution.py:603
  40.6 2.5 %expand.2 = bf16[32,192,128]{2,1,0:T(8,128)(2,1)} custom-call(bf16[8,192,128]{2,1,0:T(8,128)(2,1)S(1)} %all_to_all.35.sent_ref), custom_call_target="tpu_custom_call" | custom-call | tf_op jit(solution)/shard_map/expand/pallas_call | solution.py:217
  43.1 22.0 %all-to-all-done.2.rows_ref.refs_0_ = bf16[32,208,128]{2,1,0:T(8,128)(2,1)S(1)} async-done(((bf16[32,208,128]{2,1,0:T(8,128)(2,1)}), bf16[32,208,128]{2,1,0:T(8,128)(2,1)S(1)}, u32[]{:S(2)}, u32[]{:S(2)}) %all-to-all-start.2) | async-done | bytes 1703968 | tf_op jit(solution)/shard_map/all_to_all | solution.py:603
  65.2 5.5 %all-to-all-start.1 = ((bf16[32,192,128]{2,1,0:T(8,128)(2,1)}), bf16[32,192,128]{2,1,0:T(8,128)(2,1)}, u32[]{:S(2)}, u32[]{:S(2)}) async-start(bf16[32,192,128]{2,1,0:T(8,128)(2,1)} %expand.2), calls=%async_computation.1 | async-start | bytes 3145728 | tf_op jit(solution)/shard_map/all_to_all | solution.py:603
  71.3 2.8 %collective-permute-start.4 = (bf16[144,1024]{1,0:T(8,128)(2,1)S(1)}, bf16[144,1024]{1,0:T(8,128)(2,1)}, u32[]{:S(2)}, u32[]{:S(2)}) collective-permute-start(bf16[144,1024]{1,0:T(8,128)(2,1)S(1)} %get-tuple-element.18.refs_0_), channel_id=1, source_target_pairs={{0,160},{32,192},{64,224},{96,0},{128,32},{160,64},{192,96},{224,1... | collective-permute-start | bytes 884744 | tf_op jit(solution)/shard_map/ppermute | solution.py:623
  74.1 2.3 %collective-permute-start.3 = (bf16[144,1024]{1,0:T(8,128)(2,1)S(1)}, bf16[144,1024]{1,0:T(8,128)(2,1)}, u32[]{:S(2)}, u32[]{:S(2)}) collective-permute-start(bf16[144,1024]{1,0:T(8,128)(2,1)S(1)} %get-tuple-element.18.refs_0_), channel_id=1, source_target_pairs={{0,128},{32,160},{64,192},{96,224},{128,0},{160,32},{192,64},{224,... | collective-permute-start | bytes 884744 | tf_op jit(solution)/shard_map/ppermute | solution.py:623
  76.4 2.4 %collective-permute-start.2 = (bf16[144,1024]{1,0:T(8,128)(2,1)S(1)}, bf16[144,1024]{1,0:T(8,128)(2,1)}, u32[]{:S(2)}, u32[]{:S(2)}) collective-permute-start(bf16[144,1024]{1,0:T(8,128)(2,1)S(1)} %get-tuple-element.18.refs_0_), channel_id=1, source_target_pairs={{0,96},{32,128},{64,160},{96,192},{128,224},{160,0},{192,32},{224,... | collective-permute-start | bytes 884744 | tf_op jit(solution)/shard_map/ppermute | solution.py:623
  79.0 1.1 collective-permute-start.1
  80.1 13.1 %collective-permute-done.5.refs_6_ = bf16[144,1024]{1,0:T(8,128)(2,1)S(1)} collective-permute-done((bf16[144,1024]{1,0:T(8,128)(2,1)S(1)}, bf16[144,1024]{1,0:T(8,128)(2,1)S(1)}, u32[]{:S(2)}, u32[]{:S(2)}) %collective-permute-start.5) | collective-permute-done | bytes 294944 | tf_op jit(solution)/shard_map/ppermute | solution.py:623
  94.1 1.6 copy-done.4
  95.7 11.2 %gather_rows.1.refs_1_ = bf16[8,32,48,128]{3,2,1,0:T(8,128)(2,1)S(1)} custom-call(s32[256,128]{1,0:T(8,128)S(1)} %get-tuple-element.16.row_ref, bf16[8192,128]{1,0:T(8,128)(2,1)S(1)} %bitcast.17), custom_call_target="tpu_custom_call" | custom-call | tf_op jit(solution)/shard_map/gather_rows/pallas_call | solution.py:269
  106.9 1.3 dots.2.refs_2_
  108.6 3.2 %dots.3 = f32[256,128]{1,0:T(8,128)S(1)} custom-call(bf16[32,192,128]{2,1,0:T(8,128)(2,1)} %all-to-all-done.1.refs_0_.rows_ref, bf16[8,32,48,128]{3,2,1,0:T(8,128)(2,1)} %copy-done, f32[128,128]{1,0:T(8,128)S(1)} %dots.2.refs_2_), custom_call_target="tpu_custom_call" | custom-call | tf_op jit(solution)/shard_map/dots/pallas_call | solution.py:312
  112.5 10.9 %all-to-all-start.3 = ((f32[32,8,128]{2,1,0:T(8,128)}), f32[32,8,128]{2,1,0:T(8,128)S(1)}, u32[]{:S(2)}, u32[]{:S(2)}) async-start(f32[32,8,128]{2,1,0:T(8,128)} %bitcast.19), calls=%async_computation.3 | async-start | bytes 262144 | tf_op jit(solution)/shard_map/all_to_all | solution.py:603
  123.4 5.4 %collective-permute-done.refs_1_ = bf16[144,1024]{1,0:T(8,128)(2,1)} collective-permute-done((bf16[144,1024]{1,0:T(8,128)(2,1)S(1)}, bf16[144,1024]{1,0:T(8,128)(2,1)}, u32[]{:S(2)}, u32[]{:S(2)}) %collective-permute-start) | collective-permute-done | bytes 294944 | tf_op jit(solution)/shard_map/ppermute | solution.py:623
  128.8 2.1 all-to-all-done.3.ret_ref
  131.0 1.0 copy-done.6
  131.9 1.0 copy-done.8
  132.9 1.8 dscore.1
  134.7 17.9 %all_to_all.36.ds_ref = f32[8,64,128]{2,1,0:T(8,128)S(1)} all-to-all(f32[8,64,128]{2,1,0:T(8,128)S(1)} %dscore.1), channel_id=1, replica_groups=mesh['dp'=8,'table_0'=4,'table_1'=4,'table_2'=2] {'dp'}, dimensions={0} | all-to-all | bytes 524288 | tf_op jit(solution)/shard_map/all_to_all | solution.py:603
  152.6 3.1 %key_terms.1 = f32[32,8,256]{2,1,0:T(8,128)} custom-call(s32[1]{0:T(128)} %bitcast.me_ref, f32[8,64,128]{2,1,0:T(8,128)S(1)} %all_to_all.36.ds_ref, bf16[144,1024]{1,0:T(8,128)(2,1)S(1)} %get-tuple-element.18.refs_0_, bf16[144,1024]{1,0:T(8,128)(2,1)} %collective-permute-done.refs_1_, bf16[144,1024]{1,0:T(8,128)(2,1)} %collective-permute-done.1.refs_2_, ...), custom_call_target="tpu_custom_call" | custom-call | tf_op jit(solution)/shard_map/key_terms/pallas_call | solution.py:592
  155.8 5.3 %all-to-all-start.5 = ((f32[32,8,256]{2,1,0:T(8,128)}), f32[32,8,256]{2,1,0:T(8,128)S(1)}, u32[]{:S(2)}, u32[]{:S(2)}) async-start(f32[32,8,256]{2,1,0:T(8,128)} %key_terms.1), calls=%async_computation.5 | async-start | bytes 524288 | tf_op jit(solution)/shard_map/all_to_all | solution.py:603
  161.1 3.4 %weigh.2.refs_0_ = f32[12288,128]{1,0:T(8,128)} custom-call(f32[256,128]{1,0:T(8,128)S(1)} %copy-done.10, bf16[32,208,128]{2,1,0:T(8,128)(2,1)S(1)} %copy-done.3), custom_call_target="tpu_custom_call" | custom-call | tf_op jit(solution)/shard_map/weigh/pallas_call | solution.py:337
  164.5 4.7 %weigh.3.wide_ref = f32[12288,128]{1,0:T(8,128)} custom-call(f32[256,128]{1,0:T(8,128)S(1)} %copy-done.10, bf16[32,192,128]{2,1,0:T(8,128)(2,1)} %all-to-all-done.1.refs_0_.rows_ref, f32[12288,128]{1,0:T(8,128)} %weigh.2.refs_0_), custom_call_target="tpu_custom_call", output_to_operand_aliasing={{}: (2, {})} | custom-call | tf_op jit(solution)/shard_map/weigh/pallas_call | solution.py:337
  169.2 18.9 %scatter_rows.1 = (f32[8192,128]{1,0:T(8,128)}, f32[8,128]{1,0:T(8,128)S(1)}) custom-call(s32[256,128]{1,0:T(8,128)S(1)} %copy-done.13, f32[12288,128]{1,0:T(8,128)} %weigh.3.wide_ref), custom_call_target="tpu_custom_call" | custom-call | tf_op jit(solution)/shard_map/scatter_rows/pallas_call | solution.py:395
  189.5 19.5 %all_to_all.37 = f32[128,1,128]{2,1,0:T(1,128)S(1)} all-to-all(f32[128,1,128]{2,1,0:T(1,128)S(1)} %broadcast_in_dim.9), channel_id=1, replica_groups=mesh['dp'=8,'table_0'=4,'table_1'=4,'table_2'=2] {'dp','table_0','table_1'}, dimensions={0} | all-to-all | bytes 131072 | tf_op jit(solution)/shard_map/all_to_all | solution.py:603
  209.0 4.1 %scale.1 = (f32[8192,128]{1,0:T(8,128)}, f32[2,2,2,256]{3,2,1,0:T(2,128)}, f32[1,128]{1,0:T(1,128)}) custom-call(f32[128,128]{1,0:T(8,128)S(1)} %bitcast.20, f32[8,256]{1,0:T(8,128)S(1)} %get-tuple-element.22.part_ref, f32[8192,128]{1,0:T(8,128)} %get-tuple-element.23.value_ref), custom_call_target="tpu_custom_call" | custom-call | tf_op jit(solution)/shard_map/scale/pallas_call | solution.py:469
  (46 shorter events, 5.4 us)
Async XLA Ops:
  1.6 1.0 copy-start.14
  2.6 0.7 copy-start.15
  3.3 0.7 copy-start.16
  31.4 33.7 %all-to-all-start.2 = ((bf16[32,208,128]{2,1,0:T(8,128)(2,1)}), bf16[32,208,128]{2,1,0:T(8,128)(2,1)S(1)}, u32[]{:S(2)}, u32[]{:S(2)}) async-start(bf16[32,208,128]{2,1,0:T(8,128)(2,1)} %expand.3), calls=%async_computation.2 | async-start | bytes 3407872 | tf_op jit(solution)/shard_map/all_to_all | solution.py:603
  65.2 28.9 %copy-start.1 = (bf16[32,208,128]{2,1,0:T(8,128)(2,1)}, bf16[32,208,128]{2,1,0:T(8,128)(2,1)S(1)}, u32[]{:S(2)}) copy-start(bf16[32,208,128]{2,1,0:T(8,128)(2,1)S(1)} %all-to-all-done.2.rows_ref.refs_0_) | copy-start | bytes 5111812
  65.2 43.1 %all-to-all-start.1 = ((bf16[32,192,128]{2,1,0:T(8,128)(2,1)}), bf16[32,192,128]{2,1,0:T(8,128)(2,1)}, u32[]{:S(2)}, u32[]{:S(2)}) async-start(bf16[32,192,128]{2,1,0:T(8,128)(2,1)} %expand.2), calls=%async_computation.1 | async-start | bytes 3145728 | tf_op jit(solution)/shard_map/all_to_all | solution.py:603
  70.7 8.3 %collective-permute-start.6 = (bf16[144,1024]{1,0:T(8,128)(2,1)S(1)}, bf16[144,1024]{1,0:T(8,128)(2,1)S(1)}, u32[]{:S(2)}, u32[]{:S(2)}) collective-permute-start(bf16[144,1024]{1,0:T(8,128)(2,1)S(1)} %get-tuple-element.18.refs_0_), channel_id=1, source_target_pairs={{0,224},{32,0},{64,32},{96,64},{128,96},{160,128},{192,160},{224,1... | collective-permute-start | bytes 884744 | tf_op jit(solution)/shard_map/ppermute | solution.py:623
  70.8 22.4 %collective-permute-start.5 = (bf16[144,1024]{1,0:T(8,128)(2,1)S(1)}, bf16[144,1024]{1,0:T(8,128)(2,1)S(1)}, u32[]{:S(2)}, u32[]{:S(2)}) collective-permute-start(bf16[144,1024]{1,0:T(8,128)(2,1)S(1)} %get-tuple-element.18.refs_0_), channel_id=1, source_target_pairs={{0,192},{32,224},{64,0},{96,32},{128,64},{160,96},{192,128},{224,1... | collective-permute-start | bytes 884744 | tf_op jit(solution)/shard_map/ppermute | solution.py:623
  71.3 52.0 %collective-permute-start.4 = (bf16[144,1024]{1,0:T(8,128)(2,1)S(1)}, bf16[144,1024]{1,0:T(8,128)(2,1)}, u32[]{:S(2)}, u32[]{:S(2)}) collective-permute-start(bf16[144,1024]{1,0:T(8,128)(2,1)S(1)} %get-tuple-element.18.refs_0_), channel_id=1, source_target_pairs={{0,160},{32,192},{64,224},{96,0},{128,32},{160,64},{192,96},{224,1... | collective-permute-start | bytes 884744 | tf_op jit(solution)/shard_map/ppermute | solution.py:623
  74.1 49.3 %collective-permute-start.3 = (bf16[144,1024]{1,0:T(8,128)(2,1)S(1)}, bf16[144,1024]{1,0:T(8,128)(2,1)}, u32[]{:S(2)}, u32[]{:S(2)}) collective-permute-start(bf16[144,1024]{1,0:T(8,128)(2,1)S(1)} %get-tuple-element.18.refs_0_), channel_id=1, source_target_pairs={{0,128},{32,160},{64,192},{96,224},{128,0},{160,32},{192,64},{224,... | collective-permute-start | bytes 884744 | tf_op jit(solution)/shard_map/ppermute | solution.py:623
  76.4 47.0 %collective-permute-start.2 = (bf16[144,1024]{1,0:T(8,128)(2,1)S(1)}, bf16[144,1024]{1,0:T(8,128)(2,1)}, u32[]{:S(2)}, u32[]{:S(2)}) collective-permute-start(bf16[144,1024]{1,0:T(8,128)(2,1)S(1)} %get-tuple-element.18.refs_0_), channel_id=1, source_target_pairs={{0,96},{32,128},{64,160},{96,192},{128,224},{160,0},{192,32},{224,... | collective-permute-start | bytes 884744 | tf_op jit(solution)/shard_map/ppermute | solution.py:623
  79.0 15.0 %copy-start.5 = (bf16[144,1024]{1,0:T(8,128)(2,1)}, bf16[144,1024]{1,0:T(8,128)(2,1)S(1)}, u32[]{:S(2)}) copy-start(bf16[144,1024]{1,0:T(8,128)(2,1)S(1)} %collective-permute-done.6.refs_7_) | copy-start | bytes 884740
  79.0 44.4 %collective-permute-start.1 = (bf16[144,1024]{1,0:T(8,128)(2,1)S(1)}, bf16[144,1024]{1,0:T(8,128)(2,1)}, u32[]{:S(2)}, u32[]{:S(2)}) collective-permute-start(bf16[144,1024]{1,0:T(8,128)(2,1)S(1)} %get-tuple-element.18.refs_0_), channel_id=1, source_target_pairs={{0,64},{32,96},{64,128},{96,160},{128,192},{160,224},{192,0},{224,... | collective-permute-start | bytes 884744 | tf_op jit(solution)/shard_map/ppermute | solution.py:623
  93.2 0.8 copy-start.7
  93.2 35.6 %collective-permute-start = (bf16[144,1024]{1,0:T(8,128)(2,1)S(1)}, bf16[144,1024]{1,0:T(8,128)(2,1)}, u32[]{:S(2)}, u32[]{:S(2)}) collective-permute-start(bf16[144,1024]{1,0:T(8,128)(2,1)S(1)} %get-tuple-element.18.refs_0_), channel_id=1, source_target_pairs={{0,32},{32,64},{64,96},{96,128},{128,160},{160,192},{192,224},{224... | collective-permute-start | bytes 884744 | tf_op jit(solution)/shard_map/ppermute | solution.py:623
  93.4 0.7 copy-start.9
  94.0 12.9 %copy-start.12 = (s32[256,128]{1,0:T(8,128)}, s32[256,128]{1,0:T(8,128)S(1)}, u32[]{:S(2)}) copy-start(s32[256,128]{1,0:T(8,128)S(1)} %get-tuple-element.16.row_ref) | copy-start | bytes 393220
  94.0 1.6 copy-start.4
  95.7 11.2 %copy-start.2 = (bf16[32,208,128]{2,1,0:T(8,128)(2,1)S(1)}, bf16[32,208,128]{2,1,0:T(8,128)(2,1)}, u32[]{:S(2)}) copy-start(bf16[32,208,128]{2,1,0:T(8,128)(2,1)} %copy-done.1) | copy-start | bytes 5111812
  106.9 1.7 copy-start
  111.8 0.7 copy-start.11
  112.5 18.5 %all-to-all-start.3 = ((f32[32,8,128]{2,1,0:T(8,128)}), f32[32,8,128]{2,1,0:T(8,128)S(1)}, u32[]{:S(2)}, u32[]{:S(2)}) async-start(f32[32,8,128]{2,1,0:T(8,128)} %bitcast.19), calls=%async_computation.3 | async-start | bytes 262144 | tf_op jit(solution)/shard_map/all_to_all | solution.py:603
  131.0 1.0 copy-start.6
  131.9 1.0 copy-start.8
  132.9 28.2 %copy-start.3 = (bf16[32,208,128]{2,1,0:T(8,128)(2,1)S(1)}, bf16[32,208,128]{2,1,0:T(8,128)(2,1)}, u32[]{:S(2)}) copy-start(bf16[32,208,128]{2,1,0:T(8,128)(2,1)} %copy-done.1) | copy-start | bytes 5111812
  132.9 28.2 %copy-start.10 = (f32[256,128]{1,0:T(8,128)S(1)}, f32[256,128]{1,0:T(8,128)}, u32[]{:S(2)}) copy-start(f32[256,128]{1,0:T(8,128)} %copy-done.9) | copy-start | bytes 393220
  155.8 32.4 %all-to-all-start.5 = ((f32[32,8,256]{2,1,0:T(8,128)}), f32[32,8,256]{2,1,0:T(8,128)S(1)}, u32[]{:S(2)}, u32[]{:S(2)}) async-start(f32[32,8,256]{2,1,0:T(8,128)} %key_terms.1), calls=%async_computation.5 | async-start | bytes 524288 | tf_op jit(solution)/shard_map/all_to_all | solution.py:603
  164.5 4.7 %copy-start.13 = (s32[256,128]{1,0:T(8,128)S(1)}, s32[256,128]{1,0:T(8,128)}, u32[]{:S(2)}) copy-start(s32[256,128]{1,0:T(8,128)} %copy-done.12) | copy-start | bytes 393220
  188.3 1.2 collective-permute-start.7

commit v3 on v2

--- a/solution.py
+++ b/solution.py
@@ -319,7 +319,7 @@
         + [pl.BlockSpec((DOT_OWN * PART, TOK), lambda g: (g, 0))] * len(earlier),
         out_specs=pl.BlockSpec((count, TOK), lambda g: (g, 0)),
         out_shape=shape((count * steps, TOK), F32),
-        compiler_params=PARAMS if part == 0 else WIDE_PARAMS,
+        compiler_params=PARAMS,
         name="dots",
     )(rows, value, *earlier)
 
@@ -350,11 +350,21 @@
     )(weight, rows, *earlier)
 
 
-def scatter_kernel(row_ref, wide_ref, out_ref, sq_ref, *accs):
+def scatter_kernel(row_ref, wide_ref, out_ref, sq_ref, even_ref, odd_ref, come, *accs):
     step = pl.program_id(0)
+    tables = (even_ref, odd_ref)
+
+    def fetch(which, block):
+        at = pl.multiple_of((block * 2 + which) * OWN, OWN)
+        return pltpu.make_async_copy(
+            row_ref.at[pl.ds(at, OWN), :], tables[which], come.at[which]
+        )
 
     @pl.when(step == 0)
     def _():
+        fetch(0, step).start()
+        fetch(1, step).start()
+
         def clear(i, carry):
             at = pl.multiple_of(i * 64, 64)
             for acc in accs:
@@ -363,19 +373,26 @@
 
         lax.fori_loop(0, ROWS // 64, clear, 0)
 
-    waiting = []
-    for t in range(OWN):
-        for b in range(0, CAP, BATCH):
-            made = []
-            for j in range(b, b + BATCH):
-                acc = accs[j % ACCS]
-                row = row_ref[t, j]
-                made.append((acc, row, acc[pl.ds(row, 1), :] + wide_ref[pl.ds(t * CAP + j, 1), :]))
-            for acc, row, total in waiting:
-                acc[pl.ds(row, 1), :] = total
-            waiting = made
-    for acc, row, total in waiting:
-        acc[pl.ds(row, 1), :] = total
+    for which in range(2):
+        fetch(which, step).wait()
+        waiting = []
+        for t in range(OWN):
+            for b in range(0, CAP, BATCH):
+                made = []
+                for j in range(b, b + BATCH):
+                    acc = accs[j % ACCS]
+                    row = tables[which][t, j]
+                    at = (which * OWN + t) * CAP + j
+                    made.append((acc, row, acc[pl.ds(row, 1), :] + wide_ref[at : at + 1, :]))
+                for acc, row, total in waiting:
+                    acc[pl.ds(row, 1), :] = total
+                waiting = made
+        for acc, row, total in waiting:
+            acc[pl.ds(row, 1), :] = total
+
+        @pl.when(step < pl.num_programs(0) - 1)
+        def _():
+            fetch(which, step + 1).start()
 
     @pl.when(step == pl.num_programs(0) - 1)
     def _():
@@ -394,14 +411,19 @@
 def scatter_rows(row, wide):
     return pl.pallas_call(
         scatter_kernel,
-        grid=(NDP,),
+        grid=(NDP // 2,),
         in_specs=[
-            pl.BlockSpec((OWN, TOK), lambda g: (g, 0), memory_space=pltpu.SMEM),
-            pl.BlockSpec((OWN * CAP, TOK), lambda g: (g, 0)),
+            pl.BlockSpec(memory_space=pltpu.HBM),
+            pl.BlockSpec((2 * OWN * CAP, TOK), lambda g: (g, 0)),
         ],
         out_specs=vmem(2),
         out_shape=(shape((ROWS, TOK), F32), shape((8, TOK), F32)),
-        scratch_shapes=[pltpu.VMEM((ROWS, TOK), F32) for _ in range(ACCS)],
+        scratch_shapes=[
+            pltpu.SMEM((OWN, TOK), jnp.int32),
+            pltpu.SMEM((OWN, TOK), jnp.int32),
+            pltpu.SemaphoreType.DMA((2,)),
+        ]
+        + [pltpu.VMEM((ROWS, TOK), F32) for _ in range(ACCS)],
         compiler_params=WIDE_PARAMS,
         name="scatter_rows",
     )(row, wide)

time: 214 us -> 213 us (level)
    unnamed x35 -> x33, local copies, waits for them, and re-layouts: 8.48 us -> 8.17 us
where the time goes in v3:
time: 213 us; the launch traced here: 212 us
  blocking collectives  59.7 us (28%)
  Pallas kernels  58.8 us (28%)
  waiting for transfers between devices  43.9 us (21%)
  starting transfers between devices  40.7 us (19%)
  local copies, waits for them, and re-layouts  8.21 us (4%)
    all_to_all x3, blocking collectives, exchange(): return lax.all_to_all(x, axis, 0, 0, tiled=True)  59.7 us
    all_to_all x4, starting transfers between devices, exchange(): return lax.all_to_all(x, axis, 0, 0, tiled=True)  31.2 us
    all_to_all x4, waiting for transfers between devices, exchange(): return lax.all_to_all(x, axis, 0, 0, tiled=True)  23.6 us
    ppermute x7, waiting for transfers between devices, body(): lax.ppermute(late, 'dp', [(i, (i + k) % NDP) for i in range(NDP)])  19.3 us
    pallas_call x1, Pallas kernels, scatter_rows(): pl.pallas_call(scatter_kernel, grid=(NDP // 2,), in_specs=[pl.BlockSpec(m...  18.1 us
    pallas_call x1, Pallas kernels, gather_rows(): pl.pallas_call(gather_kernel, grid=(NDP,), in_specs=[pl.BlockSpec((OWN, T...  11.2 us
    ppermute x7, starting transfers between devices, body(): lax.ppermute(late, 'dp', [(i, (i + k) % NDP) for i in range(NDP)])  9.19 us
    unnamed x33, local copies, waits for them, and re-layouts  8.17 us
  transfers between devices with their start and end apart: 12, of which 6 were waited for; matrix products, arithmetic and copies ran while one was open for 0% of the time, Pallas kernels for 21%

profile of v3, /device:TPU:1, one launch (start us, length us, event | category | flops | bytes accessed | tf_op | source)
XLA Modules:
  0.0 212.2 jit_solution(1550705533802754181)
XLA Ops:
  0.6 1.0 copy.10
  1.6 0.9 copy-done.13
  3.9 2.5 %prep.1 = (bf16[8,192,128]{2,1,0:T(8,128)(2,1)S(1)}, bf16[144,1024]{1,0:T(8,128)(2,1)S(1)}) custom-call(bf16[128,1024]{1,0:T(8,128)(2,1)S(1)} %bitcast.18, bf16[2,2,512,256]{3,2,1,0:T(8,128)(2,1)} %keys_ref.1, s32[8,128]{1,0:T(8,128)S(1)} %bitcast.21, s32[8,128]{1,0:T(8,128)S(1)} %bitcast.22, bf16[128,1024]{1,0:T(8,128)(2,1)S(1)} %copy-done.13), custom_call_target="tpu_custom_call" | custom-call | tf_op jit(solution)/shard_map/prep/pallas_call | solution.py:160
  6.5 22.4 %all_to_all.35.sent_ref = bf16[8,192,128]{2,1,0:T(8,128)(2,1)S(1)} all-to-all(bf16[8,192,128]{2,1,0:T(8,128)(2,1)S(1)} %get-tuple-element.15), channel_id=1, replica_groups=mesh['dp'=8,'table_0'=4,'table_1'=4,'table_2'=2] {'dp'}, dimensions={0} | all-to-all | bytes 786432 | tf_op jit(solution)/shard_map/all_to_all | solution.py:625
  28.8 2.6 %expand.3 = bf16[32,208,128]{2,1,0:T(8,128)(2,1)} custom-call(bf16[8,192,128]{2,1,0:T(8,128)(2,1)S(1)} %all_to_all.35.sent_ref), custom_call_target="tpu_custom_call" | custom-call | tf_op jit(solution)/shard_map/expand/pallas_call | solution.py:217
  31.4 9.2 %all-to-all-start.2 = ((bf16[32,208,128]{2,1,0:T(8,128)(2,1)}), bf16[32,208,128]{2,1,0:T(8,128)(2,1)S(1)}, u32[]{:S(2)}, u32[]{:S(2)}) async-start(bf16[32,208,128]{2,1,0:T(8,128)(2,1)} %expand.3), calls=%async_computation.2 | async-start | bytes 3407872 | tf_op jit(solution)/shard_map/all_to_all | solution.py:625
  40.6 2.5 %expand.2 = bf16[32,192,128]{2,1,0:T(8,128)(2,1)} custom-call(bf16[8,192,128]{2,1,0:T(8,128)(2,1)S(1)} %all_to_all.35.sent_ref), custom_call_target="tpu_custom_call" | custom-call | tf_op jit(solution)/shard_map/expand/pallas_call | solution.py:217
  43.1 22.0 %all-to-all-done.2.rows_ref.refs_0_ = bf16[32,208,128]{2,1,0:T(8,128)(2,1)S(1)} async-done(((bf16[32,208,128]{2,1,0:T(8,128)(2,1)}), bf16[32,208,128]{2,1,0:T(8,128)(2,1)S(1)}, u32[]{:S(2)}, u32[]{:S(2)}) %all-to-all-start.2) | async-done | bytes 1703968 | tf_op jit(solution)/shard_map/all_to_all | solution.py:625
  65.2 5.5 %all-to-all-start.1 = ((bf16[32,192,128]{2,1,0:T(8,128)(2,1)}), bf16[32,192,128]{2,1,0:T(8,128)(2,1)}, u32[]{:S(2)}, u32[]{:S(2)}) async-start(bf16[32,192,128]{2,1,0:T(8,128)(2,1)} %expand.2), calls=%async_computation.1 | async-start | bytes 3145728 | tf_op jit(solution)/shard_map/all_to_all | solution.py:625
  71.3 2.8 %collective-permute-start.4 = (bf16[144,1024]{1,0:T(8,128)(2,1)S(1)}, bf16[144,1024]{1,0:T(8,128)(2,1)}, u32[]{:S(2)}, u32[]{:S(2)}) collective-permute-start(bf16[144,1024]{1,0:T(8,128)(2,1)S(1)} %get-tuple-element.18.refs_0_), channel_id=1, source_target_pairs={{0,160},{32,192},{64,224},{96,0},{128,32},{160,64},{192,96},{224,1... | collective-permute-start | bytes 884744 | tf_op jit(solution)/shard_map/ppermute | solution.py:645
  74.1 2.3 %collective-permute-start.3 = (bf16[144,1024]{1,0:T(8,128)(2,1)S(1)}, bf16[144,1024]{1,0:T(8,128)(2,1)}, u32[]{:S(2)}, u32[]{:S(2)}) collective-permute-start(bf16[144,1024]{1,0:T(8,128)(2,1)S(1)} %get-tuple-element.18.refs_0_), channel_id=1, source_target_pairs={{0,128},{32,160},{64,192},{96,224},{128,0},{160,32},{192,64},{224,... | collective-permute-start | bytes 884744 | tf_op jit(solution)/shard_map/ppermute | solution.py:645
  76.4 2.4 %collective-permute-start.2 = (bf16[144,1024]{1,0:T(8,128)(2,1)S(1)}, bf16[144,1024]{1,0:T(8,128)(2,1)}, u32[]{:S(2)}, u32[]{:S(2)}) collective-permute-start(bf16[144,1024]{1,0:T(8,128)(2,1)S(1)} %get-tuple-element.18.refs_0_), channel_id=1, source_target_pairs={{0,96},{32,128},{64,160},{96,192},{128,224},{160,0},{192,32},{224,... | collective-permute-start | bytes 884744 | tf_op jit(solution)/shard_map/ppermute | solution.py:645
  79.0 1.1 collective-permute-start.1
  80.1 13.1 %collective-permute-done.5.refs_6_ = bf16[144,1024]{1,0:T(8,128)(2,1)S(1)} collective-permute-done((bf16[144,1024]{1,0:T(8,128)(2,1)S(1)}, bf16[144,1024]{1,0:T(8,128)(2,1)S(1)}, u32[]{:S(2)}, u32[]{:S(2)}) %collective-permute-start.5) | collective-permute-done | bytes 294944 | tf_op jit(solution)/shard_map/ppermute | solution.py:645
  94.0 1.6 copy-done.3
  95.7 11.2 %gather_rows.1.refs_1_ = bf16[8,32,48,128]{3,2,1,0:T(8,128)(2,1)S(1)} custom-call(s32[256,128]{1,0:T(8,128)S(1)} %get-tuple-element.16.row_ref, bf16[8192,128]{1,0:T(8,128)(2,1)S(1)} %bitcast.17), custom_call_target="tpu_custom_call" | custom-call | tf_op jit(solution)/shard_map/gather_rows/pallas_call | solution.py:269
  106.9 1.3 dots.2.refs_2_
  108.3 3.0 %dots.3 = f32[256,128]{1,0:T(8,128)S(1)} custom-call(bf16[32,192,128]{2,1,0:T(8,128)(2,1)} %all-to-all-done.1.refs_0_.rows_ref, bf16[8,32,48,128]{3,2,1,0:T(8,128)(2,1)S(1)} %gather_rows.1.refs_1_, f32[128,128]{1,0:T(8,128)S(1)} %dots.2.refs_2_), custom_call_target="tpu_custom_call" | custom-call | tf_op jit(solution)/shard_map/dots/pallas_call | solution.py:312
  111.9 10.9 %all-to-all-start.3 = ((f32[32,8,128]{2,1,0:T(8,128)}), f32[32,8,128]{2,1,0:T(8,128)S(1)}, u32[]{:S(2)}, u32[]{:S(2)}) async-start(f32[32,8,128]{2,1,0:T(8,128)} %bitcast.19), calls=%async_computation.3 | async-start | bytes 262144 | tf_op jit(solution)/shard_map/all_to_all | solution.py:625
  122.9 6.0 %collective-permute-done.refs_1_ = bf16[144,1024]{1,0:T(8,128)(2,1)} collective-permute-done((bf16[144,1024]{1,0:T(8,128)(2,1)S(1)}, bf16[144,1024]{1,0:T(8,128)(2,1)}, u32[]{:S(2)}, u32[]{:S(2)}) %collective-permute-start) | collective-permute-done | bytes 294944 | tf_op jit(solution)/shard_map/ppermute | solution.py:645
  128.8 1.6 all-to-all-done.3.ret_ref
  130.4 1.0 copy-done.5
  131.4 1.0 copy-done.7
  132.3 1.8 dscore.1
  134.2 17.9 %all_to_all.36.ds_ref = f32[8,64,128]{2,1,0:T(8,128)S(1)} all-to-all(f32[8,64,128]{2,1,0:T(8,128)S(1)} %dscore.1), channel_id=1, replica_groups=mesh['dp'=8,'table_0'=4,'table_1'=4,'table_2'=2] {'dp'}, dimensions={0} | all-to-all | bytes 524288 | tf_op jit(solution)/shard_map/all_to_all | solution.py:625
  152.0 3.1 %key_terms.1 = f32[32,8,256]{2,1,0:T(8,128)} custom-call(s32[1]{0:T(128)} %bitcast.me_ref, f32[8,64,128]{2,1,0:T(8,128)S(1)} %all_to_all.36.ds_ref, bf16[144,1024]{1,0:T(8,128)(2,1)S(1)} %get-tuple-element.18.refs_0_, bf16[144,1024]{1,0:T(8,128)(2,1)} %collective-permute-done.refs_1_, bf16[144,1024]{1,0:T(8,128)(2,1)} %collective-permute-done.1.refs_2_, ...), custom_call_target="tpu_custom_call" | custom-call | tf_op jit(solution)/shard_map/key_terms/pallas_call | solution.py:614
  155.2 5.7 %all-to-all-start.5 = ((f32[32,8,256]{2,1,0:T(8,128)}), f32[32,8,256]{2,1,0:T(8,128)S(1)}, u32[]{:S(2)}, u32[]{:S(2)}) async-start(f32[32,8,256]{2,1,0:T(8,128)} %key_terms.1), calls=%async_computation.5 | async-start | bytes 524288 | tf_op jit(solution)/shard_map/all_to_all | solution.py:625
  160.9 3.4 %weigh.2.refs_0_ = f32[12288,128]{1,0:T(8,128)} custom-call(f32[256,128]{1,0:T(8,128)S(1)} %copy-done.9, bf16[32,208,128]{2,1,0:T(8,128)(2,1)S(1)} %copy-done.2), custom_call_target="tpu_custom_call" | custom-call | tf_op jit(solution)/shard_map/weigh/pallas_call | solution.py:337
  164.3 4.7 %weigh.3.wide_ref = f32[12288,128]{1,0:T(8,128)} custom-call(f32[256,128]{1,0:T(8,128)S(1)} %copy-done.9, bf16[32,192,128]{2,1,0:T(8,128)(2,1)} %all-to-all-done.1.refs_0_.rows_ref, f32[12288,128]{1,0:T(8,128)} %weigh.2.refs_0_), custom_call_target="tpu_custom_call", output_to_operand_aliasing={{}: (2, {})} | custom-call | tf_op jit(solution)/shard_map/weigh/pallas_call | solution.py:337
  169.0 18.1 %scatter_rows.1 = (f32[8192,128]{1,0:T(8,128)}, f32[8,128]{1,0:T(8,128)S(1)}) custom-call(s32[256,128]{1,0:T(8,128)S(1)} %copy-done.12, f32[12288,128]{1,0:T(8,128)} %weigh.3.wide_ref), custom_call_target="tpu_custom_call" | custom-call | tf_op jit(solution)/shard_map/scatter_rows/pallas_call | solution.py:412
  188.5 19.4 %all_to_all.37 = f32[128,1,128]{2,1,0:T(1,128)S(1)} all-to-all(f32[128,1,128]{2,1,0:T(1,128)S(1)} %broadcast_in_dim.9), channel_id=1, replica_groups=mesh['dp'=8,'table_0'=4,'table_1'=4,'table_2'=2] {'dp','table_0','table_1'}, dimensions={0} | all-to-all | bytes 131072 | tf_op jit(solution)/shard_map/all_to_all | solution.py:625
  207.9 4.1 %scale.1 = (f32[8192,128]{1,0:T(8,128)}, f32[2,2,2,256]{3,2,1,0:T(2,128)}, f32[1,128]{1,0:T(1,128)}) custom-call(f32[128,128]{1,0:T(8,128)S(1)} %bitcast.20, f32[8,256]{1,0:T(8,128)S(1)} %get-tuple-element.22.part_ref, f32[8192,128]{1,0:T(8,128)} %get-tuple-element.23.value_ref), custom_call_target="tpu_custom_call" | custom-call | tf_op jit(solution)/shard_map/scale/pallas_call | solution.py:491
  (44 shorter events, 5.1 us)
Async XLA Ops:
  1.6 1.0 copy-start.13
  2.6 0.7 copy-start.14
  3.3 0.7 copy-start.15
  31.4 33.7 %all-to-all-start.2 = ((bf16[32,208,128]{2,1,0:T(8,128)(2,1)}), bf16[32,208,128]{2,1,0:T(8,128)(2,1)S(1)}, u32[]{:S(2)}, u32[]{:S(2)}) async-start(bf16[32,208,128]{2,1,0:T(8,128)(2,1)} %expand.3), calls=%async_computation.2 | async-start | bytes 3407872 | tf_op jit(solution)/shard_map/all_to_all | solution.py:625
  65.2 28.9 %copy-start = (bf16[32,208,128]{2,1,0:T(8,128)(2,1)}, bf16[32,208,128]{2,1,0:T(8,128)(2,1)S(1)}, u32[]{:S(2)}) copy-start(bf16[32,208,128]{2,1,0:T(8,128)(2,1)S(1)} %all-to-all-done.2.rows_ref.refs_0_) | copy-start | bytes 5111812
  65.2 43.1 %all-to-all-start.1 = ((bf16[32,192,128]{2,1,0:T(8,128)(2,1)}), bf16[32,192,128]{2,1,0:T(8,128)(2,1)}, u32[]{:S(2)}, u32[]{:S(2)}) async-start(bf16[32,192,128]{2,1,0:T(8,128)(2,1)} %expand.2), calls=%async_computation.1 | async-start | bytes 3145728 | tf_op jit(solution)/shard_map/all_to_all | solution.py:625
  70.7 8.3 %collective-permute-start.6 = (bf16[144,1024]{1,0:T(8,128)(2,1)S(1)}, bf16[144,1024]{1,0:T(8,128)(2,1)S(1)}, u32[]{:S(2)}, u32[]{:S(2)}) collective-permute-start(bf16[144,1024]{1,0:T(8,128)(2,1)S(1)} %get-tuple-element.18.refs_0_), channel_id=1, source_target_pairs={{0,224},{32,0},{64,32},{96,64},{128,96},{160,128},{192,160},{224,1... | collective-permute-start | bytes 884744 | tf_op jit(solution)/shard_map/ppermute | solution.py:645
  70.8 22.4 %collective-permute-start.5 = (bf16[144,1024]{1,0:T(8,128)(2,1)S(1)}, bf16[144,1024]{1,0:T(8,128)(2,1)S(1)}, u32[]{:S(2)}, u32[]{:S(2)}) collective-permute-start(bf16[144,1024]{1,0:T(8,128)(2,1)S(1)} %get-tuple-element.18.refs_0_), channel_id=1, source_target_pairs={{0,192},{32,224},{64,0},{96,32},{128,64},{160,96},{192,128},{224,1... | collective-permute-start | bytes 884744 | tf_op jit(solution)/shard_map/ppermute | solution.py:645
  71.3 51.5 %collective-permute-start.4 = (bf16[144,1024]{1,0:T(8,128)(2,1)S(1)}, bf16[144,1024]{1,0:T(8,128)(2,1)}, u32[]{:S(2)}, u32[]{:S(2)}) collective-permute-start(bf16[144,1024]{1,0:T(8,128)(2,1)S(1)} %get-tuple-element.18.refs_0_), channel_id=1, source_target_pairs={{0,160},{32,192},{64,224},{96,0},{128,32},{160,64},{192,96},{224,1... | collective-permute-start | bytes 884744 | tf_op jit(solution)/shard_map/ppermute | solution.py:645
  74.1 48.7 %collective-permute-start.3 = (bf16[144,1024]{1,0:T(8,128)(2,1)S(1)}, bf16[144,1024]{1,0:T(8,128)(2,1)}, u32[]{:S(2)}, u32[]{:S(2)}) collective-permute-start(bf16[144,1024]{1,0:T(8,128)(2,1)S(1)} %get-tuple-element.18.refs_0_), channel_id=1, source_target_pairs={{0,128},{32,160},{64,192},{96,224},{128,0},{160,32},{192,64},{224,... | collective-permute-start | bytes 884744 | tf_op jit(solution)/shard_map/ppermute | solution.py:645
  76.4 46.4 %collective-permute-start.2 = (bf16[144,1024]{1,0:T(8,128)(2,1)S(1)}, bf16[144,1024]{1,0:T(8,128)(2,1)}, u32[]{:S(2)}, u32[]{:S(2)}) collective-permute-start(bf16[144,1024]{1,0:T(8,128)(2,1)S(1)} %get-tuple-element.18.refs_0_), channel_id=1, source_target_pairs={{0,96},{32,128},{64,160},{96,192},{128,224},{160,0},{192,32},{224,... | collective-permute-start | bytes 884744 | tf_op jit(solution)/shard_map/ppermute | solution.py:645
  79.0 15.0 %copy-start.4 = (bf16[144,1024]{1,0:T(8,128)(2,1)}, bf16[144,1024]{1,0:T(8,128)(2,1)S(1)}, u32[]{:S(2)}) copy-start(bf16[144,1024]{1,0:T(8,128)(2,1)S(1)} %collective-permute-done.6.refs_7_) | copy-start | bytes 884740
  79.0 43.8 %collective-permute-start.1 = (bf16[144,1024]{1,0:T(8,128)(2,1)S(1)}, bf16[144,1024]{1,0:T(8,128)(2,1)}, u32[]{:S(2)}, u32[]{:S(2)}) collective-permute-start(bf16[144,1024]{1,0:T(8,128)(2,1)S(1)} %get-tuple-element.18.refs_0_), channel_id=1, source_target_pairs={{0,64},{32,96},{64,128},{96,160},{128,192},{160,224},{192,0},{224,... | collective-permute-start | bytes 884744 | tf_op jit(solution)/shard_map/ppermute | solution.py:645
  93.2 0.8 copy-start.6
  93.2 35.6 %collective-permute-start = (bf16[144,1024]{1,0:T(8,128)(2,1)S(1)}, bf16[144,1024]{1,0:T(8,128)(2,1)}, u32[]{:S(2)}, u32[]{:S(2)}) collective-permute-start(bf16[144,1024]{1,0:T(8,128)(2,1)S(1)} %get-tuple-element.18.refs_0_), channel_id=1, source_target_pairs={{0,32},{32,64},{64,96},{96,128},{128,160},{160,192},{192,224},{224... | collective-permute-start | bytes 884744 | tf_op jit(solution)/shard_map/ppermute | solution.py:645
  93.4 0.7 copy-start.8
  94.0 12.9 %copy-start.11 = (s32[256,128]{1,0:T(8,128)}, s32[256,128]{1,0:T(8,128)S(1)}, u32[]{:S(2)}) copy-start(s32[256,128]{1,0:T(8,128)S(1)} %get-tuple-element.16.row_ref) | copy-start | bytes 393220
  94.0 1.6 copy-start.3
  95.7 11.2 %copy-start.1 = (bf16[32,208,128]{2,1,0:T(8,128)(2,1)S(1)}, bf16[32,208,128]{2,1,0:T(8,128)(2,1)}, u32[]{:S(2)}) copy-start(bf16[32,208,128]{2,1,0:T(8,128)(2,1)} %copy-done) | copy-start | bytes 5111812
  111.2 0.6 copy-start.10
  111.9 18.5 %all-to-all-start.3 = ((f32[32,8,128]{2,1,0:T(8,128)}), f32[32,8,128]{2,1,0:T(8,128)S(1)}, u32[]{:S(2)}, u32[]{:S(2)}) async-start(f32[32,8,128]{2,1,0:T(8,128)} %bitcast.19), calls=%async_computation.3 | async-start | bytes 262144 | tf_op jit(solution)/shard_map/all_to_all | solution.py:625
  130.4 1.0 copy-start.5
  131.4 1.0 copy-start.7
  132.3 28.5 %copy-start.2 = (bf16[32,208,128]{2,1,0:T(8,128)(2,1)S(1)}, bf16[32,208,128]{2,1,0:T(8,128)(2,1)}, u32[]{:S(2)}) copy-start(bf16[32,208,128]{2,1,0:T(8,128)(2,1)} %copy-done) | copy-start | bytes 5111812
  132.3 28.5 %copy-start.9 = (f32[256,128]{1,0:T(8,128)S(1)}, f32[256,128]{1,0:T(8,128)}, u32[]{:S(2)}) copy-start(f32[256,128]{1,0:T(8,128)} %copy-done.8) | copy-start | bytes 393220
  155.2 32.0 %all-to-all-start.5 = ((f32[32,8,256]{2,1,0:T(8,128)}), f32[32,8,256]{2,1,0:T(8,128)S(1)}, u32[]{:S(2)}, u32[]{:S(2)}) async-start(f32[32,8,256]{2,1,0:T(8,128)} %key_terms.1), calls=%async_computation.5 | async-start | bytes 524288 | tf_op jit(solution)/shard_map/all_to_all | solution.py:625
  164.3 4.7 %copy-start.12 = (s32[256,128]{1,0:T(8,128)S(1)}, s32[256,128]{1,0:T(8,128)}, u32[]{:S(2)}) copy-start(s32[256,128]{1,0:T(8,128)} %copy-done.11) | copy-start | bytes 393220
  187.3 1.2 collective-permute-start.7

commit v4 on v3

--- a/solution.py
+++ b/solution.py
@@ -29,6 +29,7 @@
 ACCS = 8
 BATCH = 4
 EXTRA = 16
+CHUNKS = 8
 F32 = jnp.float32
 BF16 = jnp.bfloat16
 LIMIT_RATIO = 5.0
@@ -350,7 +351,7 @@
     )(weight, rows, *earlier)
 
 
-def scatter_kernel(row_ref, wide_ref, out_ref, sq_ref, even_ref, odd_ref, come, *accs):
+def scatter_kernel(row_ref, wide_ref, out_ref, sq_ref, even_ref, odd_ref, come, go, *accs):
     step = pl.program_id(0)
     tables = (even_ref, odd_ref)
 
@@ -396,16 +397,28 @@
 
     @pl.when(step == pl.num_programs(0) - 1)
     def _():
-        def collect(i, total):
-            at = pl.multiple_of(i * 64, 64)
-            value = accs[0][pl.ds(at, 64), :]
-            for acc in accs[1:]:
-                value = value + acc[pl.ds(at, 64), :]
-            out_ref[pl.ds(at, 64), :] = value
-            square = value * value
-            return total + jnp.sum(square.reshape(8, 8, TOK), axis=0)
-
-        sq_ref[...] = lax.fori_loop(0, ROWS // 64, collect, jnp.zeros((8, TOK), F32))
+        size = ROWS // CHUNKS
+        sum_ref = accs[0]
+        square_sum = jnp.zeros((8, TOK), F32)
+        writes = []
+        for c in range(CHUNKS):
+
+            def collect(i, total):
+                at = pl.multiple_of(c * size + i * 64, 64)
+                value = sum_ref[pl.ds(at, 64), :]
+                for acc in accs[1:]:
+                    value = value + acc[pl.ds(at, 64), :]
+                sum_ref[pl.ds(at, 64), :] = value
+                square = value * value
+                return total + jnp.sum(square.reshape(8, 8, TOK), axis=0)
+
+            square_sum = lax.fori_loop(0, size // 64, collect, square_sum)
+            part = pl.ds(c * size, size)
+            writes.append(pltpu.make_async_copy(sum_ref.at[part, :], out_ref.at[part, :], go.at[c]))
+            writes[c].start()
+        sq_ref[...] = square_sum
+        for write in writes:
+            write.wait()
 
 
 def scatter_rows(row, wide):
@@ -416,12 +429,13 @@
             pl.BlockSpec(memory_space=pltpu.HBM),
             pl.BlockSpec((2 * OWN * CAP, TOK), lambda g: (g, 0)),
         ],
-        out_specs=vmem(2),
+        out_specs=[pl.BlockSpec(memory_space=pl.ANY)] + vmem(1),
         out_shape=(shape((ROWS, TOK), F32), shape((8, TOK), F32)),
         scratch_shapes=[
             pltpu.SMEM((OWN, TOK), jnp.int32),
             pltpu.SMEM((OWN, TOK), jnp.int32),
             pltpu.SemaphoreType.DMA((2,)),
+            pltpu.SemaphoreType.DMA((CHUNKS,)),
         ]
         + [pltpu.VMEM((ROWS, TOK), F32) for _ in range(ACCS)],
         compiler_params=WIDE_PARAMS,
@@ -449,9 +463,6 @@
         compiler_params=PARAMS,
         name="finish",
     )(key_pieces, value_sq)
-
-
-CHUNKS = 8
 
 
 def scale_kernel(limit, sums_ref, part_ref, value_ref, out_ref, key_ref, clip_ref, buf, come, go):

time: 213 us -> 212 us (level)
  no operation moved by 1% of the time
where the time goes in v4:
time: 212 us; the launch traced here: 211 us
  blocking collectives  59.7 us (28%)
  Pallas kernels  57.7 us (27%)
  waiting for transfers between devices  43.9 us (21%)
  starting transfers between devices  40.7 us (19%)
  local copies, waits for them, and re-layouts  8.21 us (4%)
    all_to_all x3, blocking collectives, exchange(): return lax.all_to_all(x, axis, 0, 0, tiled=True)  59.7 us
    all_to_all x4, starting transfers between devices, exchange(): return lax.all_to_all(x, axis, 0, 0, tiled=True)  31.2 us
    all_to_all x4, waiting for transfers between devices, exchange(): return lax.all_to_all(x, axis, 0, 0, tiled=True)  23.6 us
    ppermute x7, waiting for transfers between devices, body(): lax.ppermute(late, 'dp', [(i, (i + k) % NDP) for i in range(NDP)])  19.3 us
    pallas_call x1, Pallas kernels, scatter_rows(): pl.pallas_call(scatter_kernel, grid=(NDP // 2,), in_specs=[pl.BlockSpec(m...  17 us
    pallas_call x1, Pallas kernels, gather_rows(): pl.pallas_call(gather_kernel, grid=(NDP,), in_specs=[pl.BlockSpec((OWN, T...  11.2 us
    ppermute x7, starting transfers between devices, body(): lax.ppermute(late, 'dp', [(i, (i + k) % NDP) for i in range(NDP)])  9.19 us
    unnamed x33, local copies, waits for them, and re-layouts  8.17 us
  transfers between devices with their start and end apart: 12, of which 6 were waited for; matrix products, arithmetic and copies ran while one was open for 0% of the time, Pallas kernels for 21%

profile of v4, /device:TPU:1, one launch (start us, length us, event | category | flops | bytes accessed | tf_op | source)
XLA Modules:
  0.0 211.1 jit_solution(13672054108895783840)
XLA Ops:
  0.6 1.0 copy.10
  1.6 0.9 copy-done.13
  3.9 2.5 %prep.1 = (bf16[8,192,128]{2,1,0:T(8,128)(2,1)S(1)}, bf16[144,1024]{1,0:T(8,128)(2,1)S(1)}) custom-call(bf16[128,1024]{1,0:T(8,128)(2,1)S(1)} %bitcast.18, bf16[2,2,512,256]{3,2,1,0:T(8,128)(2,1)} %keys_ref.1, s32[8,128]{1,0:T(8,128)S(1)} %bitcast.21, s32[8,128]{1,0:T(8,128)S(1)} %bitcast.22, bf16[128,1024]{1,0:T(8,128)(2,1)S(1)} %copy-done.13), custom_call_target="tpu_custom_call" | custom-call | tf_op jit(solution)/shard_map/prep/pallas_call | solution.py:161
  6.5 22.4 %all_to_all.35.sent_ref = bf16[8,192,128]{2,1,0:T(8,128)(2,1)S(1)} all-to-all(bf16[8,192,128]{2,1,0:T(8,128)(2,1)S(1)} %get-tuple-element.15), channel_id=1, replica_groups=mesh['dp'=8,'table_0'=4,'table_1'=4,'table_2'=2] {'dp'}, dimensions={0} | all-to-all | bytes 786432 | tf_op jit(solution)/shard_map/all_to_all | solution.py:636
  28.8 2.6 %expand.3 = bf16[32,208,128]{2,1,0:T(8,128)(2,1)} custom-call(bf16[8,192,128]{2,1,0:T(8,128)(2,1)S(1)} %all_to_all.35.sent_ref), custom_call_target="tpu_custom_call" | custom-call | tf_op jit(solution)/shard_map/expand/pallas_call | solution.py:218
  31.4 9.2 %all-to-all-start.2 = ((bf16[32,208,128]{2,1,0:T(8,128)(2,1)}), bf16[32,208,128]{2,1,0:T(8,128)(2,1)S(1)}, u32[]{:S(2)}, u32[]{:S(2)}) async-start(bf16[32,208,128]{2,1,0:T(8,128)(2,1)} %expand.3), calls=%async_computation.2 | async-start | bytes 3407872 | tf_op jit(solution)/shard_map/all_to_all | solution.py:636
  40.6 2.5 %expand.2 = bf16[32,192,128]{2,1,0:T(8,128)(2,1)} custom-call(bf16[8,192,128]{2,1,0:T(8,128)(2,1)S(1)} %all_to_all.35.sent_ref), custom_call_target="tpu_custom_call" | custom-call | tf_op jit(solution)/shard_map/expand/pallas_call | solution.py:218
  43.1 22.0 %all-to-all-done.2.rows_ref.refs_0_ = bf16[32,208,128]{2,1,0:T(8,128)(2,1)S(1)} async-done(((bf16[32,208,128]{2,1,0:T(8,128)(2,1)}), bf16[32,208,128]{2,1,0:T(8,128)(2,1)S(1)}, u32[]{:S(2)}, u32[]{:S(2)}) %all-to-all-start.2) | async-done | bytes 1703968 | tf_op jit(solution)/shard_map/all_to_all | solution.py:636
  65.2 5.5 %all-to-all-start.1 = ((bf16[32,192,128]{2,1,0:T(8,128)(2,1)}), bf16[32,192,128]{2,1,0:T(8,128)(2,1)}, u32[]{:S(2)}, u32[]{:S(2)}) async-start(bf16[32,192,128]{2,1,0:T(8,128)(2,1)} %expand.2), calls=%async_computation.1 | async-start | bytes 3145728 | tf_op jit(solution)/shard_map/all_to_all | solution.py:636
  71.3 2.8 %collective-permute-start.4 = (bf16[144,1024]{1,0:T(8,128)(2,1)S(1)}, bf16[144,1024]{1,0:T(8,128)(2,1)}, u32[]{:S(2)}, u32[]{:S(2)}) collective-permute-start(bf16[144,1024]{1,0:T(8,128)(2,1)S(1)} %get-tuple-element.18.refs_0_), channel_id=1, source_target_pairs={{0,160},{32,192},{64,224},{96,0},{128,32},{160,64},{192,96},{224,1... | collective-permute-start | bytes 884744 | tf_op jit(solution)/shard_map/ppermute | solution.py:656
  74.1 2.3 %collective-permute-start.3 = (bf16[144,1024]{1,0:T(8,128)(2,1)S(1)}, bf16[144,1024]{1,0:T(8,128)(2,1)}, u32[]{:S(2)}, u32[]{:S(2)}) collective-permute-start(bf16[144,1024]{1,0:T(8,128)(2,1)S(1)} %get-tuple-element.18.refs_0_), channel_id=1, source_target_pairs={{0,128},{32,160},{64,192},{96,224},{128,0},{160,32},{192,64},{224,... | collective-permute-start | bytes 884744 | tf_op jit(solution)/shard_map/ppermute | solution.py:656
  76.4 2.4 %collective-permute-start.2 = (bf16[144,1024]{1,0:T(8,128)(2,1)S(1)}, bf16[144,1024]{1,0:T(8,128)(2,1)}, u32[]{:S(2)}, u32[]{:S(2)}) collective-permute-start(bf16[144,1024]{1,0:T(8,128)(2,1)S(1)} %get-tuple-element.18.refs_0_), channel_id=1, source_target_pairs={{0,96},{32,128},{64,160},{96,192},{128,224},{160,0},{192,32},{224,... | collective-permute-start | bytes 884744 | tf_op jit(solution)/shard_map/ppermute | solution.py:656
  79.0 1.1 collective-permute-start.1
  80.1 13.1 %collective-permute-done.5.refs_6_ = bf16[144,1024]{1,0:T(8,128)(2,1)S(1)} collective-permute-done((bf16[144,1024]{1,0:T(8,128)(2,1)S(1)}, bf16[144,1024]{1,0:T(8,128)(2,1)S(1)}, u32[]{:S(2)}, u32[]{:S(2)}) %collective-permute-start.5) | collective-permute-done | bytes 294944 | tf_op jit(solution)/shard_map/ppermute | solution.py:656
  94.0 1.6 copy-done.3
  95.7 11.2 %gather_rows.1.refs_1_ = bf16[8,32,48,128]{3,2,1,0:T(8,128)(2,1)S(1)} custom-call(s32[256,128]{1,0:T(8,128)S(1)} %get-tuple-element.16.row_ref, bf16[8192,128]{1,0:T(8,128)(2,1)S(1)} %bitcast.17), custom_call_target="tpu_custom_call" | custom-call | tf_op jit(solution)/shard_map/gather_rows/pallas_call | solution.py:270
  106.9 1.3 dots.2.refs_2_
  108.3 3.0 %dots.3 = f32[256,128]{1,0:T(8,128)S(1)} custom-call(bf16[32,192,128]{2,1,0:T(8,128)(2,1)} %all-to-all-done.1.refs_0_.rows_ref, bf16[8,32,48,128]{3,2,1,0:T(8,128)(2,1)S(1)} %gather_rows.1.refs_1_, f32[128,128]{1,0:T(8,128)S(1)} %dots.2.refs_2_), custom_call_target="tpu_custom_call" | custom-call | tf_op jit(solution)/shard_map/dots/pallas_call | solution.py:313
  111.9 10.9 %all-to-all-start.3 = ((f32[32,8,128]{2,1,0:T(8,128)}), f32[32,8,128]{2,1,0:T(8,128)S(1)}, u32[]{:S(2)}, u32[]{:S(2)}) async-start(f32[32,8,128]{2,1,0:T(8,128)} %bitcast.19), calls=%async_computation.3 | async-start | bytes 262144 | tf_op jit(solution)/shard_map/all_to_all | solution.py:636
  122.9 6.0 %collective-permute-done.refs_1_ = bf16[144,1024]{1,0:T(8,128)(2,1)} collective-permute-done((bf16[144,1024]{1,0:T(8,128)(2,1)S(1)}, bf16[144,1024]{1,0:T(8,128)(2,1)}, u32[]{:S(2)}, u32[]{:S(2)}) %collective-permute-start) | collective-permute-done | bytes 294944 | tf_op jit(solution)/shard_map/ppermute | solution.py:656
  128.8 1.6 all-to-all-done.3.ret_ref
  130.4 1.0 copy-done.5
  131.4 1.0 copy-done.7
  132.3 1.8 dscore.1
  134.2 17.9 %all_to_all.36.ds_ref = f32[8,64,128]{2,1,0:T(8,128)S(1)} all-to-all(f32[8,64,128]{2,1,0:T(8,128)S(1)} %dscore.1), channel_id=1, replica_groups=mesh['dp'=8,'table_0'=4,'table_1'=4,'table_2'=2] {'dp'}, dimensions={0} | all-to-all | bytes 524288 | tf_op jit(solution)/shard_map/all_to_all | solution.py:636
  152.0 3.1 %key_terms.1 = f32[32,8,256]{2,1,0:T(8,128)} custom-call(s32[1]{0:T(128)} %bitcast.me_ref, f32[8,64,128]{2,1,0:T(8,128)S(1)} %all_to_all.36.ds_ref, bf16[144,1024]{1,0:T(8,128)(2,1)S(1)} %get-tuple-element.18.refs_0_, bf16[144,1024]{1,0:T(8,128)(2,1)} %collective-permute-done.refs_1_, bf16[144,1024]{1,0:T(8,128)(2,1)} %collective-permute-done.1.refs_2_, ...), custom_call_target="tpu_custom_call" | custom-call | tf_op jit(solution)/shard_map/key_terms/pallas_call | solution.py:625
  155.2 5.7 %all-to-all-start.5 = ((f32[32,8,256]{2,1,0:T(8,128)}), f32[32,8,256]{2,1,0:T(8,128)S(1)}, u32[]{:S(2)}, u32[]{:S(2)}) async-start(f32[32,8,256]{2,1,0:T(8,128)} %key_terms.1), calls=%async_computation.5 | async-start | bytes 524288 | tf_op jit(solution)/shard_map/all_to_all | solution.py:636
  160.9 3.4 %weigh.2.refs_0_ = f32[12288,128]{1,0:T(8,128)} custom-call(f32[256,128]{1,0:T(8,128)S(1)} %copy-done.9, bf16[32,208,128]{2,1,0:T(8,128)(2,1)S(1)} %copy-done.2), custom_call_target="tpu_custom_call" | custom-call | tf_op jit(solution)/shard_map/weigh/pallas_call | solution.py:338
  164.3 4.7 %weigh.3.wide_ref = f32[12288,128]{1,0:T(8,128)} custom-call(f32[256,128]{1,0:T(8,128)S(1)} %copy-done.9, bf16[32,192,128]{2,1,0:T(8,128)(2,1)} %all-to-all-done.1.refs_0_.rows_ref, f32[12288,128]{1,0:T(8,128)} %weigh.2.refs_0_), custom_call_target="tpu_custom_call", output_to_operand_aliasing={{}: (2, {})} | custom-call | tf_op jit(solution)/shard_map/weigh/pallas_call | solution.py:338
  169.0 17.0 %scatter_rows.1 = (f32[8192,128]{1,0:T(8,128)}, f32[8,128]{1,0:T(8,128)S(1)}) custom-call(s32[256,128]{1,0:T(8,128)S(1)} %copy-done.12, f32[12288,128]{1,0:T(8,128)} %weigh.3.wide_ref), custom_call_target="tpu_custom_call" | custom-call | tf_op jit(solution)/shard_map/scatter_rows/pallas_call | solution.py:425
  187.3 19.4 %all_to_all.37 = f32[128,1,128]{2,1,0:T(1,128)S(1)} all-to-all(f32[128,1,128]{2,1,0:T(1,128)S(1)} %broadcast_in_dim.9), channel_id=1, replica_groups=mesh['dp'=8,'table_0'=4,'table_1'=4,'table_2'=2] {'dp','table_0','table_1'}, dimensions={0} | all-to-all | bytes 131072 | tf_op jit(solution)/shard_map/all_to_all | solution.py:636
  206.8 4.1 %scale.1 = (f32[8192,128]{1,0:T(8,128)}, f32[2,2,2,256]{3,2,1,0:T(2,128)}, f32[1,128]{1,0:T(1,128)}) custom-call(f32[128,128]{1,0:T(8,128)S(1)} %bitcast.20, f32[8,256]{1,0:T(8,128)S(1)} %get-tuple-element.22.part_ref, f32[8192,128]{1,0:T(8,128)} %get-tuple-element.23.value_ref), custom_call_target="tpu_custom_call" | custom-call | tf_op jit(solution)/shard_map/scale/pallas_call | solution.py:502
  (44 shorter events, 5.1 us)
Async XLA Ops:
  1.6 1.0 copy-start.13
  2.6 0.7 copy-start.14
  3.3 0.7 copy-start.15
  31.4 33.7 %all-to-all-start.2 = ((bf16[32,208,128]{2,1,0:T(8,128)(2,1)}), bf16[32,208,128]{2,1,0:T(8,128)(2,1)S(1)}, u32[]{:S(2)}, u32[]{:S(2)}) async-start(bf16[32,208,128]{2,1,0:T(8,128)(2,1)} %expand.3), calls=%async_computation.2 | async-start | bytes 3407872 | tf_op jit(solution)/shard_map/all_to_all | solution.py:636
  65.2 28.9 %copy-start = (bf16[32,208,128]{2,1,0:T(8,128)(2,1)}, bf16[32,208,128]{2,1,0:T(8,128)(2,1)S(1)}, u32[]{:S(2)}) copy-start(bf16[32,208,128]{2,1,0:T(8,128)(2,1)S(1)} %all-to-all-done.2.rows_ref.refs_0_) | copy-start | bytes 5111812
  65.2 43.1 %all-to-all-start.1 = ((bf16[32,192,128]{2,1,0:T(8,128)(2,1)}), bf16[32,192,128]{2,1,0:T(8,128)(2,1)}, u32[]{:S(2)}, u32[]{:S(2)}) async-start(bf16[32,192,128]{2,1,0:T(8,128)(2,1)} %expand.2), calls=%async_computation.1 | async-start | bytes 3145728 | tf_op jit(solution)/shard_map/all_to_all | solution.py:636
  70.7 8.3 %collective-permute-start.6 = (bf16[144,1024]{1,0:T(8,128)(2,1)S(1)}, bf16[144,1024]{1,0:T(8,128)(2,1)S(1)}, u32[]{:S(2)}, u32[]{:S(2)}) collective-permute-start(bf16[144,1024]{1,0:T(8,128)(2,1)S(1)} %get-tuple-element.18.refs_0_), channel_id=1, source_target_pairs={{0,224},{32,0},{64,32},{96,64},{128,96},{160,128},{192,160},{224,1... | collective-permute-start | bytes 884744 | tf_op jit(solution)/shard_map/ppermute | solution.py:656
  70.8 22.4 %collective-permute-start.5 = (bf16[144,1024]{1,0:T(8,128)(2,1)S(1)}, bf16[144,1024]{1,0:T(8,128)(2,1)S(1)}, u32[]{:S(2)}, u32[]{:S(2)}) collective-permute-start(bf16[144,1024]{1,0:T(8,128)(2,1)S(1)} %get-tuple-element.18.refs_0_), channel_id=1, source_target_pairs={{0,192},{32,224},{64,0},{96,32},{128,64},{160,96},{192,128},{224,1... | collective-permute-start | bytes 884744 | tf_op jit(solution)/shard_map/ppermute | solution.py:656
  71.3 51.5 %collective-permute-start.4 = (bf16[144,1024]{1,0:T(8,128)(2,1)S(1)}, bf16[144,1024]{1,0:T(8,128)(2,1)}, u32[]{:S(2)}, u32[]{:S(2)}) collective-permute-start(bf16[144,1024]{1,0:T(8,128)(2,1)S(1)} %get-tuple-element.18.refs_0_), channel_id=1, source_target_pairs={{0,160},{32,192},{64,224},{96,0},{128,32},{160,64},{192,96},{224,1... | collective-permute-start | bytes 884744 | tf_op jit(solution)/shard_map/ppermute | solution.py:656
  74.1 48.7 %collective-permute-start.3 = (bf16[144,1024]{1,0:T(8,128)(2,1)S(1)}, bf16[144,1024]{1,0:T(8,128)(2,1)}, u32[]{:S(2)}, u32[]{:S(2)}) collective-permute-start(bf16[144,1024]{1,0:T(8,128)(2,1)S(1)} %get-tuple-element.18.refs_0_), channel_id=1, source_target_pairs={{0,128},{32,160},{64,192},{96,224},{128,0},{160,32},{192,64},{224,... | collective-permute-start | bytes 884744 | tf_op jit(solution)/shard_map/ppermute | solution.py:656
  76.4 46.4 %collective-permute-start.2 = (bf16[144,1024]{1,0:T(8,128)(2,1)S(1)}, bf16[144,1024]{1,0:T(8,128)(2,1)}, u32[]{:S(2)}, u32[]{:S(2)}) collective-permute-start(bf16[144,1024]{1,0:T(8,128)(2,1)S(1)} %get-tuple-element.18.refs_0_), channel_id=1, source_target_pairs={{0,96},{32,128},{64,160},{96,192},{128,224},{160,0},{192,32},{224,... | collective-permute-start | bytes 884744 | tf_op jit(solution)/shard_map/ppermute | solution.py:656
  79.0 15.0 %copy-start.4 = (bf16[144,1024]{1,0:T(8,128)(2,1)}, bf16[144,1024]{1,0:T(8,128)(2,1)S(1)}, u32[]{:S(2)}) copy-start(bf16[144,1024]{1,0:T(8,128)(2,1)S(1)} %collective-permute-done.6.refs_7_) | copy-start | bytes 884740
  79.0 43.8 %collective-permute-start.1 = (bf16[144,1024]{1,0:T(8,128)(2,1)S(1)}, bf16[144,1024]{1,0:T(8,128)(2,1)}, u32[]{:S(2)}, u32[]{:S(2)}) collective-permute-start(bf16[144,1024]{1,0:T(8,128)(2,1)S(1)} %get-tuple-element.18.refs_0_), channel_id=1, source_target_pairs={{0,64},{32,96},{64,128},{96,160},{128,192},{160,224},{192,0},{224,... | collective-permute-start | bytes 884744 | tf_op jit(solution)/shard_map/ppermute | solution.py:656
  93.2 0.8 copy-start.6
  93.2 35.6 %collective-permute-start = (bf16[144,1024]{1,0:T(8,128)(2,1)S(1)}, bf16[144,1024]{1,0:T(8,128)(2,1)}, u32[]{:S(2)}, u32[]{:S(2)}) collective-permute-start(bf16[144,1024]{1,0:T(8,128)(2,1)S(1)} %get-tuple-element.18.refs_0_), channel_id=1, source_target_pairs={{0,32},{32,64},{64,96},{96,128},{128,160},{160,192},{192,224},{224... | collective-permute-start | bytes 884744 | tf_op jit(solution)/shard_map/ppermute | solution.py:656
  93.4 0.7 copy-start.8
  94.0 12.9 %copy-start.11 = (s32[256,128]{1,0:T(8,128)}, s32[256,128]{1,0:T(8,128)S(1)}, u32[]{:S(2)}) copy-start(s32[256,128]{1,0:T(8,128)S(1)} %get-tuple-element.16.row_ref) | copy-start | bytes 393220
  94.0 1.6 copy-start.3
  95.7 11.2 %copy-start.1 = (bf16[32,208,128]{2,1,0:T(8,128)(2,1)S(1)}, bf16[32,208,128]{2,1,0:T(8,128)(2,1)}, u32[]{:S(2)}) copy-start(bf16[32,208,128]{2,1,0:T(8,128)(2,1)} %copy-done) | copy-start | bytes 5111812
  111.2 0.6 copy-start.10
  111.9 18.5 %all-to-all-start.3 = ((f32[32,8,128]{2,1,0:T(8,128)}), f32[32,8,128]{2,1,0:T(8,128)S(1)}, u32[]{:S(2)}, u32[]{:S(2)}) async-start(f32[32,8,128]{2,1,0:T(8,128)} %bitcast.19), calls=%async_computation.3 | async-start | bytes 262144 | tf_op jit(solution)/shard_map/all_to_all | solution.py:636
  130.4 1.0 copy-start.5
  131.4 1.0 copy-start.7
  132.3 28.5 %copy-start.2 = (bf16[32,208,128]{2,1,0:T(8,128)(2,1)S(1)}, bf16[32,208,128]{2,1,0:T(8,128)(2,1)}, u32[]{:S(2)}) copy-start(bf16[32,208,128]{2,1,0:T(8,128)(2,1)} %copy-done) | copy-start | bytes 5111812
  132.3 28.5 %copy-start.9 = (f32[256,128]{1,0:T(8,128)S(1)}, f32[256,128]{1,0:T(8,128)}, u32[]{:S(2)}) copy-start(f32[256,128]{1,0:T(8,128)} %copy-done.8) | copy-start | bytes 393220
  155.2 30.8 %all-to-all-start.5 = ((f32[32,8,256]{2,1,0:T(8,128)}), f32[32,8,256]{2,1,0:T(8,128)S(1)}, u32[]{:S(2)}, u32[]{:S(2)}) async-start(f32[32,8,256]{2,1,0:T(8,128)} %key_terms.1), calls=%async_computation.5 | async-start | bytes 524288 | tf_op jit(solution)/shard_map/all_to_all | solution.py:636
  164.3 4.7 %copy-start.12 = (s32[256,128]{1,0:T(8,128)S(1)}, s32[256,128]{1,0:T(8,128)}, u32[]{:S(2)}) copy-start(s32[256,128]{1,0:T(8,128)} %copy-done.11) | copy-start | bytes 393220
  186.1 1.2 collective-permute-start.7
